TPU v7x, 256 devices: a whole 4x4x8 slice. The times are simulated.
256 devices in a mesh: energy: 64 (over y, x_lo, z), layer: 4 (over x_hi, core).
Axes of the slice: x: 4 (x_hi: 2, x_lo: 2; x = x_hi * 2 + x_lo), y: 4, z: 8, core: 2. Of those that a mesh axis runs over, the one named last changes fastest.
Arguments:
- layer_inverse: float32 [64, 32, 256, 256], P('energy', 'layer'), may hold values from -0.008125 to 1, as said below
- coupling: float32 [256, 256], replicated, may hold values from -0.5125 to 0.5125, as said below
- lead_left: float32 [64, 256, 256], P('energy'), may hold values from -0.0040625 to 0.5, as said below
- lead_right: float32 [64, 256, 256], P('energy'), may hold values from -0.0040625 to 0.5, as said below
- quad_weight: float32 [64], replicated, may hold values from 0.0015625 to 0.0625
- energy_slot: int32 [64], P('energy'), may hold values from 0 to 63, each once
- plane_of: int32 [32], replicated, may hold values from 0 to 1023
- doping: float32 [1024, 128, 128], P(('energy', 'layer')), may hold values from -6 to 6
- screening: float32 [1024, 128, 128], P(('energy', 'layer')), may hold values from 0.25 to 2
Outputs:
- layer_density: float32 [32, 256], P('layer')
- potential: float32 [1024, 128, 128], P(('energy', 'layer'))
- residual: float32 [1024, 128, 128], P(('energy', 'layer'))
Inputs may be any that keep to these rules, and one draw needn't show every extreme that they name: `layer_inverse`: each block is symmetric; its diagonal entries lie between 0.3 and 1.0 and its other entries within 0.13 * 256 ** -0.5 of zero. `coupling`: entries are independent with mean zero. `lead_left`: each block is symmetric; its diagonal entries lie between 0.15 and 0.5 and its other entries within 0.065 * 256 ** -0.5 of zero. `lead_right`: each block is symmetric; its diagonal entries lie between 0.15 and 0.5 and its other entries within 0.065 * 256 ** -0.5 of zero. `energy_slot`: every quadrature index appears once. `plane_of`: several layers may share a plane.
All inputs are finite; a program needn't handle non-finite values.
Results may differ from a plain program's by a relative error of at most 0.00018.
Values sent between devices are 32-bit elements; how exact they have to be, the bound alone decides.
No kernel may reach another device: no remote copies, remote signals or barrier semaphores. Data moves between devices by JAX's collectives and lax.ppermute only.
A program may use at most 128 MiB of HBM per device.

v0:
```python
import functools

import jax
import jax.numpy as jnp
from jax import lax
from jax.experimental import pallas as pl
from jax.experimental.pallas import tpu as pltpu
from jax.sharding import Mesh
from jax.sharding import PartitionSpec as P

LAYER = ("layer_0", "layer_1")
ENERGY_LAYER = ("energy_0", "energy_1", "energy_2", "layer_0", "layer_1")
DEEP = ("energy_2",)
ACROSS = ("energy_0", "energy_1", "layer_0", "layer_1")
ENERGY = ("energy_0", "energy_1", "energy_2")

F32, BF16 = jnp.float32, jnp.bfloat16
NN = (((1,), (0,)), ((), ()))
NT = (((1,), (1,)), ((), ()))
VMEM = pl.BlockSpec(memory_space=pltpu.VMEM)
SMEM = pl.BlockSpec(memory_space=pltpu.SMEM)
HALF = 128
PACKED = 2 * HALF + 8
SHIFT = 7.125


def halves(x):
    high = x.astype(BF16)
    return high, (x - high.astype(F32)).astype(BF16)


def product(a, b, dims):
    dot = functools.partial(lax.dot_general, dimension_numbers=dims, preferred_element_type=F32)
    return dot(a[0], b[0]) + (dot(a[0], b[1]) + dot(a[1], b[0]))


def square_iota(n):
    return (lax.broadcasted_iota(jnp.int32, (n, n), 0), lax.broadcasted_iota(jnp.int32, (n, n), 1))


def diagonal_row(x):
    rows, cols = square_iota(x.shape[0])
    return jnp.sum(jnp.where(rows == cols, x, 0.0), axis=0, keepdims=True)


def pack(out_ref, x):
    rows, cols = square_iota(HALF)
    low, high = x[:HALF, :HALF], x[HALF:, HALF:]
    out_ref[:HALF, :] = x[:HALF, HALF:]
    out_ref[HALF : 2 * HALF, :] = jnp.where(rows >= cols, low, high)
    out_ref[2 * HALF :, :] = jnp.broadcast_to(diagonal_row(high), (8, HALF))


def unpack(ref, out_ref):
    rows, cols = square_iota(HALF)
    off, both = ref[:HALF, :], ref[HALF : 2 * HALF, :]
    flipped = both.T
    out_ref[:HALF, :HALF] = jnp.where(rows >= cols, both, flipped)
    out_ref[:HALF, HALF:] = off
    out_ref[HALF:, :HALF] = off.T
    high = jnp.where(rows < cols, both, flipped)
    out_ref[HALF:, HALF:] = jnp.where(rows == cols, ref[2 * HALF : 2 * HALF + 1, :], high)


def chain_kernel(
    place, d_ref, t_ref, lead_ref, lead_r_ref,
    send_ref, base_ref, state_ref, map_h, map_l, kh_ref, kl_ref,
    ph, pw,
):
    layers = d_ref.shape[0]
    coupling = halves(t_ref[...])

    @pl.loop(0, layers)
    def _(layer):
        inverse = d_ref[layer]
        split = halves(inverse)
        for side, dims in ((0, NN), (1, NT)):
            high, low = halves(product(split, coupling, dims))
            ph[side, layer] = high
            pw[side, layer] = low
        base_ref[pl.ds(layer, 1), :] = -diagonal_row(inverse)

    rows, cols = square_iota(d_ref.shape[1])
    for side, first in ((0, 0), (1, layers - 1)):
        state_ref[side] = d_ref[first]
        base_ref[first : first + 1, :] += diagonal_row(d_ref[first])
        start = (ph[side, first].astype(F32) + pw[side, first].astype(F32)).T
        kh_ref[side, first], kl_ref[side, first] = halves(start)

    @pl.loop(1, layers)
    def _(step):
        for side in (0, 1):
            layer = step if side == 0 else layers - 1 - step
            before = step - 1 if side == 0 else layers - step
            move = (ph[side, layer], pw[side, layer])
            carried = product((kh_ref[side, before], kl_ref[side, before]), move, NT)
            kh_ref[side, layer], kl_ref[side, layer] = halves(carried)
            half_way = product(move, halves(state_ref[side]), NN)
            updated = d_ref[layer] + product(halves(half_way), move, NT)
            state_ref[side] = updated
            base_ref[pl.ds(layer, 1), :] += diagonal_row(updated)

    for side, last in ((0, layers - 1), (1, 0)):
        whole = (kh_ref[side, last].astype(F32) + kl_ref[side, last].astype(F32)).T
        map_h[side], map_l[side] = halves(whole)
    side = (place[0] >= 2).astype(jnp.int32)
    entering = jnp.where(place[0] >= 2, lead_r_ref[...], lead_ref[...])
    pack(send_ref, through(entering, side, state_ref, map_h, map_l))


def through(entering, side, state_ref, map_h, map_l):
    whole = (map_h[side], map_l[side])
    half_way = product(whole, halves(entering), NN)
    return state_ref[side] + product(halves(half_way), whole, NT)


def hop_kernel(right_at, place, received_ref, state_ref, map_h, map_l, send_ref, full):
    unpack(received_ref, full)
    side = (place[0] == right_at).astype(jnp.int32)
    pack(send_ref, through(full[...], side, state_ref, map_h, map_l))


def add_corrections(side, full, base_ref, kh_ref, kl_ref, out_ref):
    entering = halves(full[...])
    for layer in range(base_ref.shape[0]):
        high, low = kh_ref[side, layer], kl_ref[side, layer]
        moved = product(entering, (high, low), NN)
        carried = high.astype(F32) + low.astype(F32)
        row = jnp.sum(moved * carried, axis=0, keepdims=True)
        out_ref[layer : layer + 1, :] = base_ref[layer : layer + 1, :] + row


def first_kernel(place, received_ref, lead_ref, lead_r_ref, base_ref, kh_ref, kl_ref, out_ref, full):
    segment = place[0]

    @pl.when(segment == 0)
    def _():
        full[...] = lead_ref[...]

    @pl.when(segment == 3)
    def _():
        full[...] = lead_r_ref[...]

    @pl.when((segment == 1) | (segment == 2))
    def _():
        unpack(received_ref, full)

    side = (segment >= 2).astype(jnp.int32)
    add_corrections(side, full, base_ref, kh_ref, kl_ref, out_ref)


def second_kernel(
    place, slot, weights, third_ref, second_ref, base_ref, kh_ref, kl_ref, out_ref, full, rows_ref
):
    segment = place[0]

    @pl.when((segment == 0) | (segment == 3))
    def _():
        unpack(third_ref, full)

    @pl.when((segment == 1) | (segment == 2))
    def _():
        unpack(second_ref, full)

    side = (segment < 2).astype(jnp.int32)
    add_corrections(side, full, base_ref, kh_ref, kl_ref, rows_ref)
    weighted = rows_ref[...] * weights[slot[0]]
    for peer in range(out_ref.shape[0]):
        out_ref[peer] = weighted


def fan_kernel(pieces_ref, out_ref):
    total = pieces_ref[0]
    for peer in range(1, pieces_ref.shape[0]):
        total = total + pieces_ref[peer]
    for peer in range(out_ref.shape[0]):
        out_ref[peer] = total


def krylov_kernel(
    place, plane_of, pieces_ref, doping_ref, screening_ref, below_ref, above_ref,
    own_rows_ref, basis_ref, sums_ref, src, one, two, density_ref,
):
    slab, last_slab = place[1], place[2]
    layers = pieces_ref.shape[1]
    segments = plane_of.shape[0] // layers
    for segment in range(segments):
        rows = pieces_ref[segment]
        for piece in range(segments + segment, pieces_ref.shape[0], segments):
            rows = rows + pieces_ref[piece]
        density_ref[segment * layers : (segment + 1) * layers, :] = rows
    own_rows_ref[...] = density_ref[pl.ds(pl.multiple_of(place[0] * layers, layers), layers), :]
    own = doping_ref.shape[0]
    depth = 3
    y_cells, z_cells = doping_ref.shape[1:]
    rows, cols = square_iota(y_cells)
    orbitals = density_ref.shape[1]
    for i in range(own + 2 * depth):
        if i < depth:
            src[i] = -below_ref[i]
        elif i < depth + own:
            src[i] = -doping_ref[i - depth]
        else:
            src[i] = -above_ref[i - depth - own]

    first_plane = slab * own - depth

    @pl.loop(0, plane_of.shape[0])
    def _(layer):
        at = plane_of[layer] - first_plane

        @pl.when((at >= 0) & (at < own + 2 * depth))
        def _():
            width = 16
            row = jnp.broadcast_to(density_ref[pl.ds(layer, 1), :], (y_cells, orbitals))
            yy = lax.broadcasted_iota(jnp.int32, (y_cells, orbitals), 0)
            mm = lax.broadcasted_iota(jnp.int32, (y_cells, orbitals), 1)
            spread = jnp.where(mm // width == yy // (y_cells // width), row, 0.0)
            zz = lax.broadcasted_iota(jnp.int32, (orbitals, z_cells), 1)
            mz = lax.broadcasted_iota(jnp.int32, (orbitals, z_cells), 0)
            pick = (mz % width == zz // (z_cells // width)).astype(F32).astype(BF16)
            high, low = halves(spread)
            lowest = (spread - high.astype(F32) - low.astype(F32)).astype(BF16)
            dot = functools.partial(
                lax.dot_general, dimension_numbers=NN, preferred_element_type=F32
            )
            src[at] = src[at] + (dot(high, pick) + (dot(low, pick) + dot(lowest, pick)))

    def screen(i):
        if i < depth:
            return below_ref[i + 2]
        if i < depth + own:
            return screening_ref[i - depth]
        return above_ref[i - own]

    def shifted_operator(ref, i):
        plane = ref[i]
        beside = ref[i - 1] + ref[i + 1]
        beside = beside + jnp.where(rows == 0, 0.0, pltpu.roll(plane, 1, 0))
        beside = beside + jnp.where(rows == y_cells - 1, 0.0, pltpu.roll(plane, y_cells - 1, 0))
        beside = beside + jnp.where(cols == 0, 0.0, pltpu.roll(plane, 1, 1))
        beside = beside + jnp.where(cols == z_cells - 1, 0.0, pltpu.roll(plane, z_cells - 1, 1))
        return (screen(i) + (6.0 - SHIFT)) * plane - beside

    inside_low = jnp.where(slab == 0, 0.0, 1.0)
    inside_high = jnp.where(slab == last_slab, 0.0, 1.0)

    def masked(i, plane):
        if i < depth:
            return plane * inside_low
        if i >= depth + own:
            return plane * inside_high
        return plane

    for i in range(1, own + 2 * depth - 1):
        one[i] = masked(i, shifted_operator(src, i))
    for i in range(2, own + 2 * depth - 2):
        two[i] = masked(i, shifted_operator(one, i))
    totals = [jnp.zeros((y_cells, z_cells), F32) for _ in range(6)]
    for i in range(depth, depth + own):
        three = shifted_operator(two, i)
        v = (src[i], one[i], two[i], three)
        for k in range(4):
            basis_ref[k, i - depth] = v[k]
        for k in range(6):
            totals[k] = totals[k] + v[k // 2] * v[k - k // 2]
    lane = lax.broadcasted_iota(jnp.int32, (1, z_cells), 1)
    out = jnp.zeros((1, z_cells), F32)
    for k in range(6):
        total = jnp.sum(jnp.sum(totals[k], axis=0, keepdims=True), axis=1, keepdims=True)
        out = out + jnp.where(lane == k, total, 0.0)
    for peer in range(sums_ref.shape[0]):
        sums_ref[peer] = out


def finish_kernel(sums_ref, basis_ref, potential_ref, residual_ref):
    total = jnp.sum(sums_ref[...], axis=0)
    lane = lax.broadcasted_iota(jnp.int32, total.shape, 1)
    m = [jnp.sum(jnp.where(lane == k, total, 0.0), axis=1, keepdims=True) for k in range(6)]

    def inner(a, b):
        terms = [x * y * m[i + j] for i, x in enumerate(a) for j, y in enumerate(b)]
        return functools.reduce(lambda p, q: p + q, terms)

    def applied(c):
        moved = [SHIFT * x for x in c] + [c[-1]]
        for i in range(len(c) - 1):
            moved[i + 1] = moved[i + 1] + c[i]
        return moved

    def plus(a, scale, b):
        n = max(len(a), len(b))
        a = list(a) + [None] * (n - len(a))
        b = list(b) + [None] * (n - len(b))
        return [
            x if y is None else (scale * y if x is None else x + scale * y) for x, y in zip(a, b)
        ]

    unit = jnp.ones_like(m[0])
    residual = [unit]
    direction = [unit]
    potential = []
    norm = m[0]
    for iteration in range(3):
        image = applied(direction)
        step = norm / inner(direction, image)
        potential = plus(potential, step, direction)
        residual = plus(residual, -step, image)
        if iteration < 2:
            following = inner(residual, residual)
            direction = plus(residual, following / norm, direction)
            norm = following
    for i in range(potential_ref.shape[0]):
        v = [basis_ref[k, i] for k in range(4)]
        potential_ref[i] = potential[0] * v[0] + potential[1] * v[1] + potential[2] * v[2]
        residual_ref[i] = (
            residual[0] * v[0] + residual[1] * v[1] + residual[2] * v[2] + residual[3] * v[3]
        )


def call(kernel, out_shape, in_specs, scratch=(), flops=0, out_specs=None, name=None):
    return pl.pallas_call(
        kernel,
        out_shape=out_shape,
        in_specs=in_specs,
        out_specs=jax.tree.map(lambda _: VMEM, out_shape) if out_specs is None else out_specs,
        scratch_shapes=list(scratch),
        name=name,
        cost_estimate=pl.CostEstimate(flops=flops, bytes_accessed=0, transcendentals=0),
        compiler_params=pltpu.CompilerParams(vmem_limit_bytes=40 * 2**20),
    )


def shape(*dims, dtype=F32):
    return jax.ShapeDtypeStruct(dims, dtype)


def exchange(copies, axis):
    return lax.all_to_all(copies, axis, 0, 0, tiled=True)


def body(
    layer_inverse, coupling, lead_left, lead_right, quad_weight, energy_slot, plane_of, doping, screening
):
    inverse, left, right = layer_inverse[0], lead_left[0], lead_right[0]
    layers, size = inverse.shape[0], inverse.shape[1]
    slab = lax.axis_index(ENERGY_LAYER)
    slabs = lax.axis_size(ENERGY_LAYER)
    place = jnp.stack([lax.axis_index(LAYER), slab, jnp.int32(slabs - 1)]).astype(jnp.int32)
    own, ny, nz = doping.shape

    up = [(i, i + 1) for i in range(slabs - 1)]
    down = [(i + 1, i) for i in range(slabs - 1)]
    below = lax.ppermute(jnp.concatenate([doping[own - 3 :], screening[own - 2 :]]), ENERGY_LAYER, up)
    above = lax.ppermute(jnp.concatenate([doping[:3], screening[:2]]), ENERGY_LAYER, down)

    send, base, state, map_h, map_l, kh, kl = call(
        chain_kernel,
        (
            shape(PACKED, HALF), shape(layers, size), shape(2, size, size),
            shape(2, size, size, dtype=BF16), shape(2, size, size, dtype=BF16),
            shape(2, layers, size, size, dtype=BF16), shape(2, layers, size, size, dtype=BF16),
        ),
        [SMEM, VMEM, VMEM, VMEM, VMEM],
        [pltpu.VMEM((2, layers, size, size), BF16)] * 2,
        flops=10**7, name="chain",
    )(place, inverse, coupling, left, right)

    def hop(received, right_at):
        return call(
            functools.partial(hop_kernel, right_at), shape(PACKED, HALF),
            [SMEM, VMEM, VMEM, VMEM, VMEM], [pltpu.VMEM((size, size), F32)],
            flops=10**6, name=f"hop_{right_at}",
        )(place, received, state, map_h, map_l)

    first = lax.ppermute(send, LAYER, [(0, 1), (3, 2)])
    second = lax.ppermute(hop(first, 2), LAYER, [(1, 2), (2, 1)])
    once = call(
        first_kernel, shape(layers, size), [SMEM] + [VMEM] * 6, [pltpu.VMEM((size, size), F32)],
        flops=10**7, name="first",
    )(place, first, left, right, base, kh, kl)
    third = lax.ppermute(hop(second, 1), LAYER, [(2, 3), (1, 0)])
    partial = call(
        second_kernel, shape(lax.axis_size(DEEP), layers, size), [SMEM] * 3 + [VMEM] * 5,
        [pltpu.VMEM((size, size), F32), pltpu.VMEM((layers, size), F32)],
        flops=10**7, name="second",
    )(place, energy_slot, quad_weight, third, second, once, kh, kl)
    along_z = exchange(partial, DEEP)
    fanned = call(
        fan_kernel, shape(lax.axis_size(ACROSS), layers, size), [VMEM], flops=10**6, name="fan"
    )(along_z)
    pieces = exchange(fanned, ACROSS)

    own_rows, basis, sums = call(
        krylov_kernel,
        (shape(layers, size), shape(4, own, ny, nz), shape(slabs, 1, nz)),
        [SMEM, SMEM] + [VMEM] * 5,
        [pltpu.VMEM((own + 6, ny, nz), F32)] * 3 + [pltpu.VMEM((plane_of.shape[0], size), F32)],
        flops=10**6, name="krylov",
    )(place, plane_of, pieces, doping, screening, below, above)
    all_sums = exchange(sums, ENERGY_LAYER)
    potential, residual = call(
        finish_kernel, (shape(own, ny, nz), shape(own, ny, nz)), [VMEM] * 2,
        flops=10**6, name="finish",
    )(all_sums, basis)
    return own_rows, potential, residual


def solution(mesh):
    split = Mesh(
        mesh.devices.reshape(4, 2, 8, 2, 2),
        ("energy_0", "energy_1", "energy_2", "layer_0", "layer_1"),
    )
    in_specs = (
        P(ENERGY, LAYER, None, None),
        P(),
        P(ENERGY, None, None),
        P(ENERGY, None, None),
        P(),
        P(ENERGY),
        P(),
        P(ENERGY_LAYER, None, None),
        P(ENERGY_LAYER, None, None),
    )
    out_specs = (P(LAYER, None), P(ENERGY_LAYER, None, None), P(ENERGY_LAYER, None, None))
    return jax.shard_map(body, mesh=split, in_specs=in_specs, out_specs=out_specs, check_vma=False)
```

profile of v0, /device:TPU:1, one launch (start us, length us, event | category | flops | bytes accessed | tf_op | source)
XLA Modules:
  0.0 96.5 jit_solution(17861226851912270996)
XLA Ops:
  0.6 0.1 pad_add_fusion.place
  0.7 0.0 copy-start
  0.7 1.6 %copy-done = f32[1,8,256,256]{3,2,1,0:T(8,128)S(1)} copy-done((f32[1,8,256,256]{3,2,1,0:T(8,128)S(1)}, f32[1,8,256,256]{3,2,1,0:T(8,128)}, u32[]{:S(2)}) %copy-start) | copy-done | bytes 2097176
  2.3 0.0 copy-start.2
  2.3 0.9 copy-done.2
  3.3 0.0 copy-start.3
  3.3 0.9 copy-done.3
  4.2 0.0 copy-start.5
  4.2 0.9 copy-done.5
  5.2 0.0 copy-start.1
  5.2 12.3 %chain.1 = (f32[264,128]{1,0:T(8,128)S(1)}, f32[8,256]{1,0:T(8,128)S(1)}, f32[2,256,256]{2,1,0:T(8,128)S(1)}, bf16[2,256,256]{2,1,0:T(8,128)(2,1)S(1)}, bf16[2,2...) custom-call(s32[3]{0:T(128)S(1)} %pad_add_fusion.place, ...), custom_call_target="tpu_custom_call" | custom-call | flops 10000000 | tf_op jit(solution)/shard_map/chain/pallas_call | solution.py:357
  17.5 0.0 copy-start.4
  17.5 1.4 %collective-permute-start = (f32[264,128]{1,0:T(8,128)S(1)}, f32[264,128]{1,0:T(8,128)S(1)}, u32[]{:S(2)}, u32[]{:S(2)}) collective-permute-start(f32[264,128]{1,0:T(8,128)S(1)} %get-tuple-element.15), channel_id=1, source_target_pairs={{0,1},{3,2},{4,5},{7,6},{8,9},{11,10},{12,13},{15,14},{16,17},{19,... | collective-permute-start | bytes 405512 | tf_op jit(solution)/shard_map/ppermute | solution.py:376
  19.0 4.0 %collective-permute-done.received_ref = f32[264,128]{1,0:T(8,128)S(1)} collective-permute-done((f32[264,128]{1,0:T(8,128)S(1)}, f32[264,128]{1,0:T(8,128)S(1)}, u32[]{:S(2)}, u32[]{:S(2)}) %collective-permute-start) | collective-permute-done | bytes 135200 | tf_op jit(solution)/shard_map/ppermute | solution.py:376
  23.0 1.2 %hop_2.1 = f32[264,128]{1,0:T(8,128)S(1)} custom-call(s32[3]{0:T(128)S(1)} %pad_add_fusion.place, f32[264,128]{1,0:T(8,128)S(1)} %collective-permute-done.received_ref, f32[2,256,256]{2,1,0:T(8,128)S(1)} %get-tuple-element.16.state_ref, bf16[2,256,256]{2,1,0:T(8,128)(2,1)S(1)} %get-tuple-element.17.map_h, bf16[2,256,256]{2,1,0:T(8,128)(2,1)S(1)} %get-tuple-element.18.map_l), custom_call_target="tpu_custom_call" | custom-call | flops 1000000 | tf_op jit(solution)/shard_map/hop_2/pallas_call | solution.py:370
  24.2 4.0 %collective-permute-start.1 = (f32[264,128]{1,0:T(8,128)S(1)}, f32[264,128]{1,0:T(8,128)S(1)}, u32[]{:S(2)}, u32[]{:S(2)}) collective-permute-start(f32[264,128]{1,0:T(8,128)S(1)} %hop_2.1), channel_id=1, source_target_pairs={{1,2},{2,1},{5,6},{6,5},{9,10},{10,9},{13,14},{14,13},{17,18},{18,... | collective-permute-start | bytes 405512 | tf_op jit(solution)/shard_map/ppermute | solution.py:377
  28.2 0.0 copy-done.1
  28.2 3.8 %collective-permute-done.1.received_ref.second_ref = f32[264,128]{1,0:T(8,128)S(1)} collective-permute-done((f32[264,128]{1,0:T(8,128)S(1)}, f32[264,128]{1,0:T(8,128)S(1)}, u32[]{:S(2)}, u32[]{:S(2)}) %collective-permute-start.1) | collective-permute-done | bytes 135200 | tf_op jit(solution)/shard_map/ppermute | solution.py:377
  32.1 1.2 %hop_1.1 = f32[264,128]{1,0:T(8,128)S(1)} custom-call(s32[3]{0:T(128)S(1)} %pad_add_fusion.place, f32[264,128]{1,0:T(8,128)S(1)} %collective-permute-done.1.received_ref.second_ref, f32[2,256,256]{2,1,0:T(8,128)S(1)} %get-tuple-element.16.state_ref, bf16[2,256,256]{2,1,0:T(8,128)(2,1)S(1)} %get-tuple-element.17.map_h, ...), custom_call_target="tpu_custom_call" | custom-call | flops 1000000 | tf_op jit(solution)/shard_map/hop_1/pallas_call | solution.py:370
  33.3 1.3 %collective-permute-start.2 = (f32[264,128]{1,0:T(8,128)S(1)}, f32[264,128]{1,0:T(8,128)S(1)}, u32[]{:S(2)}, u32[]{:S(2)}) collective-permute-start(f32[264,128]{1,0:T(8,128)S(1)} %hop_1.1), channel_id=1, source_target_pairs={{2,3},{1,0},{6,7},{5,4},{10,11},{9,8},{14,15},{13,12},{18,19},{17,... | collective-permute-start | bytes 405512 | tf_op jit(solution)/shard_map/ppermute | solution.py:382
  34.6 0.0 copy-done.4
  34.7 4.0 %collective-permute-start.3 = (f32[5,128,128]{2,1,0:T(8,128)S(1)}, f32[5,128,128]{2,1,0:T(8,128)S(1)}, u32[]{:S(2)}, u32[]{:S(2)}) collective-permute-start(f32[5,128,128]{2,1,0:T(8,128)S(1)} %pad_maximum_fusion), channel_id=1, source_target_pairs={{0,1},{1,2},{2,3},{3,4},{4,5},{5,6},{6,7},{7,8},{8,9},{9,10},{10,1... | collective-permute-start | bytes 983048 | tf_op jit(solution)/shard_map/ppermute | solution.py:354
  39.3 0.0 copy-start.7
  39.3 1.7 %first.1.base_ref = f32[8,256]{1,0:T(8,128)S(1)} custom-call(s32[3]{0:T(128)S(1)} %pad_add_fusion.place, f32[264,128]{1,0:T(8,128)S(1)} %collective-permute-done.received_ref, f32[256,256]{1,0:T(8,128)S(1)} %bitcast.7, f32[256,256]{1,0:T(8,128)S(1)} %bitcast.9, f32[8,256]{1,0:T(8,128)S(1)} %get-tuple-element.19.base_ref, ...), custom_call_target="tpu_custom_call" | custom-call | flops 10000000 | tf_op jit(solution)/shard_map/first/pallas_call | solution.py:378
  41.0 0.0 copy-start.6
  41.0 0.0 collective-permute-done.2.third_ref
  41.0 0.0 copy-done.7
  41.0 2.3 %second.1 = f32[8,8,256]{2,1,0:T(8,128)} custom-call(s32[3]{0:T(128)S(1)} %pad_add_fusion.place, s32[1]{0:T(128)S(6)} %copy.12.slot, f32[64]{0:T(128)S(1)} %copy-done.7, f32[264,128]{1,0:T(8,128)S(1)} %collective-permute-done.2.third_ref, f32[264,128]{1,0:T(8,128)S(1)} %collective-permute-done.1.received_ref.second_ref, f32[8,256]{1,0:T(8,128)S(1)} %first.1.base_ref, ...), custom_call_target="tpu_custom_call" | custom-call | flops 10000000 | tf_op jit(solution)/shard_map/second/pallas_call | solution.py:383
  43.4 8.2 %all-to-all-start = ((f32[8,8,256]{2,1,0:T(8,128)}), f32[8,8,256]{2,1,0:T(8,128)S(1)}, u32[]{:S(2)}, u32[]{:S(2)}) async-start(f32[8,8,256]{2,1,0:T(8,128)} %second.1), calls=%async_computation | async-start | bytes 131072 | tf_op jit(solution)/shard_map/all_to_all | solution.py:339
  51.6 1.9 %collective-permute-start.4 = (f32[5,128,128]{2,1,0:T(8,128)S(1)}, f32[5,128,128]{2,1,0:T(8,128)S(1)}, u32[]{:S(2)}, u32[]{:S(2)}) collective-permute-start(f32[5,128,128]{2,1,0:T(8,128)S(1)} %pad_maximum_fusion.1), channel_id=1, source_target_pairs={{1,0},{2,1},{3,2},{4,3},{5,4},{6,5},{7,6},{8,7},{9,8},{10,9},{11,1... | collective-permute-start | bytes 983048 | tf_op jit(solution)/shard_map/ppermute | solution.py:355
  53.5 5.3 %all-to-all-done.pieces_ref = f32[8,8,256]{2,1,0:T(8,128)S(1)} async-done(((f32[8,8,256]{2,1,0:T(8,128)}), f32[8,8,256]{2,1,0:T(8,128)S(1)}, u32[]{:S(2)}, u32[]{:S(2)}) %all-to-all-start) | async-done | bytes 65568 | tf_op jit(solution)/shard_map/all_to_all | solution.py:339
  58.8 0.7 fan.1
  59.5 5.9 %all-to-all-start.1 = ((f32[32,8,256]{2,1,0:T(8,128)}), f32[32,8,256]{2,1,0:T(8,128)S(1)}, u32[]{:S(2)}, u32[]{:S(2)}) async-start(f32[32,8,256]{2,1,0:T(8,128)} %fan.1), calls=%async_computation.1 | async-start | bytes 524288 | tf_op jit(solution)/shard_map/all_to_all | solution.py:339
  65.4 0.0 collective-permute-done.3.below_ref
  65.4 0.0 collective-permute-done.4.above_ref
  65.4 8.6 %all-to-all-done.1.pieces_ref = f32[32,8,256]{2,1,0:T(8,128)S(1)} async-done(((f32[32,8,256]{2,1,0:T(8,128)}), f32[32,8,256]{2,1,0:T(8,128)S(1)}, u32[]{:S(2)}, u32[]{:S(2)}) %all-to-all-start.1) | async-done | bytes 262176 | tf_op jit(solution)/shard_map/all_to_all | solution.py:339
  74.0 0.0 copy-done.6
  74.0 2.1 %krylov.1 = (f32[8,256]{1,0:T(8,128)}, f32[4,4,128,128]{3,2,1,0:T(8,128)S(1)}, f32[256,1,128]{2,1,0:T(1,128)S(1)}) custom-call(s32[3]{0:T(128)S(1)} %pad_add_fusion.place, s32[32]{0:T(128)S(1)} %copy-done.6, f32[32,8,256]{2,1,0:T(8,128)S(1)} %all-to-all-done.1.pieces_ref, f32[4,128,128]{2,1,0:T(8,128)S(1)} %copy-done.1, f32[4,128,128]{2,1,0:T(8,128)S(1)} %copy-done.4, ...), custom_call_target="tpu_custom_call" | custom-call | flops 1000000 | tf_op jit(solution)/shard_map/krylov/pallas_call | solution.py:394
  76.1 19.1 %all_to_all.15.sums_ref = f32[256,1,128]{2,1,0:T(1,128)S(1)} all-to-all(f32[256,1,128]{2,1,0:T(1,128)S(1)} %get-tuple-element.23), channel_id=1, replica_groups=mesh['energy_0'=4,'energy_1'=2,'energy_2'=8,'layer_0'=2,'layer_1'=2] {'e..., dimensions={0} | all-to-all | bytes 262144 | tf_op jit(solution)/shard_map/all_to_all | solution.py:339
  95.1 1.3 %finish.1 = (f32[4,128,128]{2,1,0:T(8,128)}, f32[4,128,128]{2,1,0:T(8,128)}) custom-call(f32[256,1,128]{2,1,0:T(1,128)S(1)} %all_to_all.15.sums_ref, f32[4,4,128,128]{3,2,1,0:T(8,128)S(1)} %get-tuple-element.24.basis_ref), custom_call_target="tpu_custom_call" | custom-call | flops 1000000 | tf_op jit(solution)/shard_map/finish/pallas_call | solution.py:402
  (4 shorter events, 0.1 us)
Async XLA Ops:
  0.7 1.6 %copy-start = (f32[1,8,256,256]{3,2,1,0:T(8,128)S(1)}, f32[1,8,256,256]{3,2,1,0:T(8,128)}, u32[]{:S(2)}) copy-start(f32[1,8,256,256]{3,2,1,0:T(8,128)} %param.9) | copy-start | bytes 6291460
  2.3 0.9 copy-start.2
  3.3 0.9 copy-start.3
  4.2 0.9 copy-start.5
  5.2 23.0 %copy-start.1 = (f32[4,128,128]{2,1,0:T(8,128)S(1)}, f32[4,128,128]{2,1,0:T(8,128)}, u32[]{:S(2)}) copy-start(f32[4,128,128]{2,1,0:T(8,128)} %doping_ref.1) | copy-start | bytes 786436
  17.5 17.1 %copy-start.4 = (f32[4,128,128]{2,1,0:T(8,128)S(1)}, f32[4,128,128]{2,1,0:T(8,128)}, u32[]{:S(2)}) copy-start(f32[4,128,128]{2,1,0:T(8,128)} %screening_ref.1) | copy-start | bytes 786436
  17.5 5.5 %collective-permute-start = (f32[264,128]{1,0:T(8,128)S(1)}, f32[264,128]{1,0:T(8,128)S(1)}, u32[]{:S(2)}, u32[]{:S(2)}) collective-permute-start(f32[264,128]{1,0:T(8,128)S(1)} %get-tuple-element.15), channel_id=1, source_target_pairs={{0,1},{3,2},{4,5},{7,6},{8,9},{11,10},{12,13},{15,14},{16,17},{19,... | collective-permute-start | bytes 405512 | tf_op jit(solution)/shard_map/ppermute | solution.py:376
  24.2 7.8 %collective-permute-start.1 = (f32[264,128]{1,0:T(8,128)S(1)}, f32[264,128]{1,0:T(8,128)S(1)}, u32[]{:S(2)}, u32[]{:S(2)}) collective-permute-start(f32[264,128]{1,0:T(8,128)S(1)} %hop_2.1), channel_id=1, source_target_pairs={{1,2},{2,1},{5,6},{6,5},{9,10},{10,9},{13,14},{14,13},{17,18},{18,... | collective-permute-start | bytes 405512 | tf_op jit(solution)/shard_map/ppermute | solution.py:377
  33.3 7.7 %collective-permute-start.2 = (f32[264,128]{1,0:T(8,128)S(1)}, f32[264,128]{1,0:T(8,128)S(1)}, u32[]{:S(2)}, u32[]{:S(2)}) collective-permute-start(f32[264,128]{1,0:T(8,128)S(1)} %hop_1.1), channel_id=1, source_target_pairs={{2,3},{1,0},{6,7},{5,4},{10,11},{9,8},{14,15},{13,12},{18,19},{17,... | collective-permute-start | bytes 405512 | tf_op jit(solution)/shard_map/ppermute | solution.py:382
  34.7 30.7 %collective-permute-start.3 = (f32[5,128,128]{2,1,0:T(8,128)S(1)}, f32[5,128,128]{2,1,0:T(8,128)S(1)}, u32[]{:S(2)}, u32[]{:S(2)}) collective-permute-start(f32[5,128,128]{2,1,0:T(8,128)S(1)} %pad_maximum_fusion), channel_id=1, source_target_pairs={{0,1},{1,2},{2,3},{3,4},{4,5},{5,6},{6,7},{7,8},{8,9},{9,10},{10,1... | collective-permute-start | bytes 983048 | tf_op jit(solution)/shard_map/ppermute | solution.py:354
  39.3 1.7 %copy-start.7 = (f32[64]{0:T(128)S(1)}, f32[64]{0:T(128)}, u32[]{:S(2)}) copy-start(f32[64]{0:T(128)} %weights.1) | copy-start | bytes 772
  41.0 33.0 %copy-start.6 = (s32[32]{0:T(128)S(1)}, s32[32]{0:T(128)}, u32[]{:S(2)}) copy-start(s32[32]{0:T(128)} %plane_of.1) | copy-start | bytes 388
  43.4 15.4 %all-to-all-start = ((f32[8,8,256]{2,1,0:T(8,128)}), f32[8,8,256]{2,1,0:T(8,128)S(1)}, u32[]{:S(2)}, u32[]{:S(2)}) async-start(f32[8,8,256]{2,1,0:T(8,128)} %second.1), calls=%async_computation | async-start | bytes 131072 | tf_op jit(solution)/shard_map/all_to_all | solution.py:339
  51.6 13.8 %collective-permute-start.4 = (f32[5,128,128]{2,1,0:T(8,128)S(1)}, f32[5,128,128]{2,1,0:T(8,128)S(1)}, u32[]{:S(2)}, u32[]{:S(2)}) collective-permute-start(f32[5,128,128]{2,1,0:T(8,128)S(1)} %pad_maximum_fusion.1), channel_id=1, source_target_pairs={{1,0},{2,1},{3,2},{4,3},{5,4},{6,5},{7,6},{8,7},{9,8},{10,9},{11,1... | collective-permute-start | bytes 983048 | tf_op jit(solution)/shard_map/ppermute | solution.py:355
  59.5 14.5 %all-to-all-start.1 = ((f32[32,8,256]{2,1,0:T(8,128)}), f32[32,8,256]{2,1,0:T(8,128)S(1)}, u32[]{:S(2)}, u32[]{:S(2)}) async-start(f32[32,8,256]{2,1,0:T(8,128)} %fan.1), calls=%async_computation.1 | async-start | bytes 524288 | tf_op jit(solution)/shard_map/all_to_all | solution.py:339
where the time goes:
time: 97 us; the launch traced here: 96.5 us
  starting transfers between devices  26.7 us (28%)
  Pallas kernels  22.9 us (24%)
  waiting for transfers between devices  21.7 us (22%)
  blocking collectives  19.1 us (20%)
  local copies, waits for them, and re-layouts  4.51 us (5%)
  between operations  1.47 us (2%)
    all_to_all x1, blocking collectives, exchange(): return lax.all_to_all(copies, axis, 0, 0, tiled=True)  19.1 us
    all_to_all x2, starting transfers between devices, exchange(): return lax.all_to_all(copies, axis, 0, 0, tiled=True)  14.1 us
    all_to_all x2, waiting for transfers between devices, exchange(): return lax.all_to_all(copies, axis, 0, 0, tiled=True)  13.9 us
    pallas_call x1, Pallas kernels, body(): call(chain_kernel, (shape(PACKED, HALF), shape(layers, size), shape(2, si...  12.3 us
    unnamed x16, local copies, waits for them, and re-layouts  4.46 us
    ppermute x1, waiting for transfers between devices, body(): first = lax.ppermute(send, LAYER, [(0, 1), (3, 2)])  4.03 us
    ppermute x1, starting transfers between devices, body(): lax.ppermute(jnp.concatenate([doping[own - 3:], screening[own - 2:]]), EN...  3.97 us
    ppermute x1, starting transfers between devices, body(): second = lax.ppermute(hop(first, 2), LAYER, [(1, 2), (2, 1)])  3.97 us
  transfers between devices with their start and end apart: 7, of which 4 were waited for; matrix products, arithmetic and copies ran while one was open for 0% of the time, Pallas kernels for 5%

commit v1 on v0

--- a/solution.py
+++ b/solution.py
@@ -18,6 +18,7 @@
 NN = (((1,), (0,)), ((), ()))
 NT = (((1,), (1,)), ((), ()))
 VMEM = pl.BlockSpec(memory_space=pltpu.VMEM)
+HBM = pl.BlockSpec(memory_space=pltpu.HBM)
 SMEM = pl.BlockSpec(memory_space=pltpu.SMEM)
 HALF = 128
 PACKED = 2 * HALF + 8
@@ -63,22 +64,38 @@
 
 
 def chain_kernel(
-    place, d_ref, t_ref, lead_ref, lead_r_ref,
+    place, d_hbm, t_hbm, lead_hbm, lead_r_hbm,
     send_ref, base_ref, state_ref, map_h, map_l, kh_ref, kl_ref,
-    ph, pw,
+    d_ref, t_ref, lead, ph, pw, arrived,
 ):
     layers = d_ref.shape[0]
+    copies = [pltpu.make_async_copy(t_hbm, t_ref, arrived.at[0])]
+    for layer in range(layers):
+        copies.append(
+            pltpu.make_async_copy(d_hbm.at[layer], d_ref.at[layer], arrived.at[1 + layer])
+        )
+    for copy in copies:
+        copy.start()
+
+    @pl.when(place[0] < 2)
+    def _():
+        pltpu.make_async_copy(lead_hbm, lead, arrived.at[1 + layers]).start()
+
+    @pl.when(place[0] >= 2)
+    def _():
+        pltpu.make_async_copy(lead_r_hbm, lead, arrived.at[1 + layers]).start()
+
+    copies[0].wait()
     coupling = halves(t_ref[...])
-
-    @pl.loop(0, layers)
-    def _(layer):
+    for layer in range(layers):
+        copies[1 + layer].wait()
         inverse = d_ref[layer]
         split = halves(inverse)
         for side, dims in ((0, NN), (1, NT)):
             high, low = halves(product(split, coupling, dims))
             ph[side, layer] = high
             pw[side, layer] = low
-        base_ref[pl.ds(layer, 1), :] = -diagonal_row(inverse)
+        base_ref[layer : layer + 1, :] = -diagonal_row(inverse)
 
     rows, cols = square_iota(d_ref.shape[1])
     for side, first in ((0, 0), (1, layers - 1)):
@@ -104,8 +121,8 @@
         whole = (kh_ref[side, last].astype(F32) + kl_ref[side, last].astype(F32)).T
         map_h[side], map_l[side] = halves(whole)
     side = (place[0] >= 2).astype(jnp.int32)
-    entering = jnp.where(place[0] >= 2, lead_r_ref[...], lead_ref[...])
-    pack(send_ref, through(entering, side, state_ref, map_h, map_l))
+    pltpu.make_async_copy(lead_hbm, lead, arrived.at[1 + layers]).wait()
+    pack(send_ref, through(lead[...], side, state_ref, map_h, map_l))
 
 
 def through(entering, side, state_ref, map_h, map_l):
@@ -130,16 +147,18 @@
         out_ref[layer : layer + 1, :] = base_ref[layer : layer + 1, :] + row
 
 
-def first_kernel(place, received_ref, lead_ref, lead_r_ref, base_ref, kh_ref, kl_ref, out_ref, full):
+def first_kernel(
+    place, received_ref, lead_hbm, lead_r_hbm, base_ref, kh_ref, kl_ref, out_ref, full
+):
     segment = place[0]
 
     @pl.when(segment == 0)
     def _():
-        full[...] = lead_ref[...]
+        pltpu.sync_copy(lead_hbm, full)
 
     @pl.when(segment == 3)
     def _():
-        full[...] = lead_r_ref[...]
+        pltpu.sync_copy(lead_r_hbm, full)
 
     @pl.when((segment == 1) | (segment == 2))
     def _():
@@ -177,8 +196,35 @@
         out_ref[peer] = total
 
 
+DEPTH = 3
+
+
+def grid_kernel(
+    place, doping_hbm, screening_hbm, below_ref, above_ref, field_ref, screen_ref, arrived
+):
+    own, planes = doping_hbm.shape[0], field_ref.shape[0]
+    copies = [
+        pltpu.make_async_copy(doping_hbm, field_ref.at[pl.ds(DEPTH, own)], arrived.at[0]),
+        pltpu.make_async_copy(screening_hbm, screen_ref.at[pl.ds(DEPTH, own)], arrived.at[1]),
+    ]
+    for copy in copies:
+        copy.start()
+    inside_low = jnp.where(place[1] == 0, 0.0, 1.0)
+    inside_high = jnp.where(place[1] == place[2], 0.0, 1.0)
+    for i in range(DEPTH):
+        field_ref[i] = below_ref[i] * -inside_low
+        field_ref[planes - DEPTH + i] = above_ref[i] * -inside_high
+    for i in range(DEPTH - 1):
+        screen_ref[i + 1] = below_ref[DEPTH + i]
+        screen_ref[planes - DEPTH + i] = above_ref[DEPTH + i]
+    for copy in copies:
+        copy.wait()
+    for i in range(DEPTH, DEPTH + own):
+        field_ref[i] = -field_ref[i]
+
+
 def krylov_kernel(
-    place, plane_of, pieces_ref, doping_ref, screening_ref, below_ref, above_ref,
+    place, plane_of, pieces_ref, field_ref, screen_ref,
     own_rows_ref, basis_ref, sums_ref, src, one, two, density_ref,
 ):
     slab, last_slab = place[1], place[2]
@@ -190,19 +236,11 @@
             rows = rows + pieces_ref[piece]
         density_ref[segment * layers : (segment + 1) * layers, :] = rows
     own_rows_ref[...] = density_ref[pl.ds(pl.multiple_of(place[0] * layers, layers), layers), :]
-    own = doping_ref.shape[0]
-    depth = 3
-    y_cells, z_cells = doping_ref.shape[1:]
+    depth, own = DEPTH, basis_ref.shape[1]
+    y_cells, z_cells = field_ref.shape[1:]
     rows, cols = square_iota(y_cells)
     orbitals = density_ref.shape[1]
-    for i in range(own + 2 * depth):
-        if i < depth:
-            src[i] = -below_ref[i]
-        elif i < depth + own:
-            src[i] = -doping_ref[i - depth]
-        else:
-            src[i] = -above_ref[i - depth - own]
-
+    src[...] = field_ref[...]
     first_plane = slab * own - depth
 
     @pl.loop(0, plane_of.shape[0])
@@ -226,13 +264,6 @@
             )
             src[at] = src[at] + (dot(high, pick) + (dot(low, pick) + dot(lowest, pick)))
 
-    def screen(i):
-        if i < depth:
-            return below_ref[i + 2]
-        if i < depth + own:
-            return screening_ref[i - depth]
-        return above_ref[i - own]
-
     def shifted_operator(ref, i):
         plane = ref[i]
         beside = ref[i - 1] + ref[i + 1]
@@ -240,7 +271,7 @@
         beside = beside + jnp.where(rows == y_cells - 1, 0.0, pltpu.roll(plane, y_cells - 1, 0))
         beside = beside + jnp.where(cols == 0, 0.0, pltpu.roll(plane, 1, 1))
         beside = beside + jnp.where(cols == z_cells - 1, 0.0, pltpu.roll(plane, z_cells - 1, 1))
-        return (screen(i) + (6.0 - SHIFT)) * plane - beside
+        return (screen_ref[i] + (6.0 - SHIFT)) * plane - beside
 
     inside_low = jnp.where(slab == 0, 0.0, 1.0)
     inside_high = jnp.where(slab == last_slab, 0.0, 1.0)
@@ -349,10 +380,14 @@
     place = jnp.stack([lax.axis_index(LAYER), slab, jnp.int32(slabs - 1)]).astype(jnp.int32)
     own, ny, nz = doping.shape
 
-    up = [(i, i + 1) for i in range(slabs - 1)]
-    down = [(i + 1, i) for i in range(slabs - 1)]
-    below = lax.ppermute(jnp.concatenate([doping[own - 3 :], screening[own - 2 :]]), ENERGY_LAYER, up)
-    above = lax.ppermute(jnp.concatenate([doping[:3], screening[:2]]), ENERGY_LAYER, down)
+    up = [(i, (i + 1) % slabs) for i in range(slabs)]
+    down = [(j, i) for i, j in up]
+    with jax.named_scope("halo_below"):
+        edge = jnp.concatenate([doping[own - 3 :], screening[own - 2 :]])
+        below = lax.ppermute(edge, ENERGY_LAYER, up)
+    with jax.named_scope("halo_above"):
+        edge = jnp.concatenate([doping[:3], screening[:2]])
+        above = lax.ppermute(edge, ENERGY_LAYER, down)
 
     send, base, state, map_h, map_l, kh, kl = call(
         chain_kernel,
@@ -361,29 +396,44 @@
             shape(2, size, size, dtype=BF16), shape(2, size, size, dtype=BF16),
             shape(2, layers, size, size, dtype=BF16), shape(2, layers, size, size, dtype=BF16),
         ),
-        [SMEM, VMEM, VMEM, VMEM, VMEM],
-        [pltpu.VMEM((2, layers, size, size), BF16)] * 2,
-        flops=10**7, name="chain",
+        [SMEM, HBM, HBM, HBM, HBM],
+        [
+            pltpu.VMEM((layers, size, size), F32), pltpu.VMEM((size, size), F32),
+            pltpu.VMEM((size, size), F32),
+            *[pltpu.VMEM((2, layers, size, size), BF16)] * 2,
+            pltpu.SemaphoreType.DMA((layers + 2,)),
+        ],
+        flops=5 * 10**9, name="chain",
     )(place, inverse, coupling, left, right)
 
     def hop(received, right_at):
         return call(
             functools.partial(hop_kernel, right_at), shape(PACKED, HALF),
             [SMEM, VMEM, VMEM, VMEM, VMEM], [pltpu.VMEM((size, size), F32)],
-            flops=10**6, name=f"hop_{right_at}",
+            flops=2 * 10**8, name=f"hop_{right_at}",
         )(place, received, state, map_h, map_l)
 
-    first = lax.ppermute(send, LAYER, [(0, 1), (3, 2)])
-    second = lax.ppermute(hop(first, 2), LAYER, [(1, 2), (2, 1)])
+    swap = [(0, 1), (1, 0), (2, 3), (3, 2)]
+    send, below, above = lax.optimization_barrier((send, below, above))
+    first = lax.ppermute(send, LAYER, swap)
+    with jax.named_scope("middle"):
+        second = lax.ppermute(hop(first, 2), LAYER, [(0, 0), (1, 2), (2, 1), (3, 3)])
+    field, screen = call(
+        grid_kernel, (shape(own + 6, ny, nz), shape(own + 6, ny, nz)),
+        [SMEM, HBM, HBM, VMEM, VMEM], [pltpu.SemaphoreType.DMA((2,))],
+        flops=2 * 10**8, name="grid",
+    )(place, doping, screening, below, above)
     once = call(
-        first_kernel, shape(layers, size), [SMEM] + [VMEM] * 6, [pltpu.VMEM((size, size), F32)],
-        flops=10**7, name="first",
+        first_kernel, shape(layers, size), [SMEM, VMEM, HBM, HBM, VMEM, VMEM, VMEM],
+        [pltpu.VMEM((size, size), F32)],
+        flops=5 * 10**8, name="first",
     )(place, first, left, right, base, kh, kl)
-    third = lax.ppermute(hop(second, 1), LAYER, [(2, 3), (1, 0)])
+    second, once, field, screen = lax.optimization_barrier((second, once, field, screen))
+    third = lax.ppermute(hop(second, 1), LAYER, swap)
     partial = call(
         second_kernel, shape(lax.axis_size(DEEP), layers, size), [SMEM] * 3 + [VMEM] * 5,
         [pltpu.VMEM((size, size), F32), pltpu.VMEM((layers, size), F32)],
-        flops=10**7, name="second",
+        flops=5 * 10**8, name="second",
     )(place, energy_slot, quad_weight, third, second, once, kh, kl)
     along_z = exchange(partial, DEEP)
     fanned = call(
@@ -394,10 +444,10 @@
     own_rows, basis, sums = call(
         krylov_kernel,
         (shape(layers, size), shape(4, own, ny, nz), shape(slabs, 1, nz)),
-        [SMEM, SMEM] + [VMEM] * 5,
+        [SMEM, SMEM] + [VMEM] * 3,
         [pltpu.VMEM((own + 6, ny, nz), F32)] * 3 + [pltpu.VMEM((plane_of.shape[0], size), F32)],
         flops=10**6, name="krylov",
-    )(place, plane_of, pieces, doping, screening, below, above)
+    )(place, plane_of, pieces, field, screen)
     all_sums = exchange(sums, ENERGY_LAYER)
     potential, residual = call(
         finish_kernel, (shape(own, ny, nz), shape(own, ny, nz)), [VMEM] * 2,

time: 97 us -> 92.1 us (0.949)
  blocking collectives: 19.1 us -> 44.4 us
  waiting for transfers between devices: 21.7 us -> 5.18 us
  starting transfers between devices: 26.7 us -> 13.5 us
  other arithmetic: 0.12 us -> 1.57 us
  local copies, waits for them, and re-layouts: 4.51 us -> 3.17 us
    all_to_all x1 -> x3, blocking collectives: 19.1 us -> 44.4 us  [exchange(): return lax.all_to_all(copies, axis, 0, 0, tiled=True)]
    all_to_all x2 -> x0, starting transfers between devices: 14.1 us -> none  [exchange(): return lax.all_to_all(copies, axis, 0, 0, tiled=True)]
    all_to_all x2 -> x0, waiting for transfers between devices: 13.9 us -> none  [exchange(): return lax.all_to_all(copies, axis, 0, 0, tiled=True)]
    unnamed x16, local copies, waits for them, and re-layouts: 4.46 us -> 0.98 us
    ppermute x5, waiting for transfers between devices: 7.85 us -> 5.18 us  [the longest x1 3.5 us: body(): lax.ppermute(hop(first, 2), LAYER, [(0, 0), (1, 2), (2, 1), (3, 3)])]
    slice x2, local copies, waits for them, and re-layouts: 0.05 us -> 2.19 us  [body(): edge = jnp.concatenate([doping[:3], screening[:2]])]
    concatenate x2, other arithmetic: 0.05 us -> 1.49 us  [the longest x1 0.75 us: body(): edge = jnp.concatenate([doping[own - 3:], screening[own - 2:]])]
    pallas_call x1 -> x2, Pallas kernels: 1.69 us -> 2.36 us  [the longest x1 1.69 us: body(): call(first_kernel, shape(layers, size), [SMEM, VMEM, HBM, HBM, VMEM, VMEM...]
  transfers between devices with their start and end apart: 7 -> 5, of which waited for: 4 -> 3; matrix products, arithmetic and copies ran while one was open for 0% -> 1% of each run, Pallas kernels for 5% -> 16%
where the time goes in v1:
time: 92.1 us; the launch traced here: 91.9 us
  blocking collectives  44.4 us (48%)
  Pallas kernels  22.6 us (25%)
  starting transfers between devices  13.5 us (15%)
  waiting for transfers between devices  5.18 us (6%)
  local copies, waits for them, and re-layouts  3.17 us (3%)
  other arithmetic  1.57 us (2%)
  between operations  1.44 us (2%)
    all_to_all x3, blocking collectives, exchange(): return lax.all_to_all(copies, axis, 0, 0, tiled=True)  44.4 us
    pallas_call x1, Pallas kernels, body(): call(chain_kernel, (shape(PACKED, HALF), shape(layers, size), shape(2, si...  12.7 us
    ppermute x1, starting transfers between devices, body(): first = lax.ppermute(send, LAYER, swap)  7.39 us
    ppermute x1, starting transfers between devices, body(): below = lax.ppermute(edge, ENERGY_LAYER, up)  4.12 us
    ppermute x1, waiting for transfers between devices, body(): lax.ppermute(hop(first, 2), LAYER, [(0, 0), (1, 2), (2, 1), (3, 3)])  3.5 us
    pallas_call x2, Pallas kernels, hop(): call(functools.partial(hop_kernel, right_at), shape(PACKED, HALF), [SMEM,...  2.47 us
    slice x2, local copies, waits for them, and re-layouts, body(): edge = jnp.concatenate([doping[:3], screening[:2]])  2.19 us
    pallas_call x1, Pallas kernels, body(): call(krylov_kernel, (shape(layers, size), shape(4, own, ny, nz), shape(sl...  2.05 us
  transfers between devices with their start and end apart: 5, of which 3 were waited for; matrix products, arithmetic and copies ran while one was open for 1% of the time, Pallas kernels for 16%

profile of v1, /device:TPU:1, one launch (start us, length us, event | category | flops | bytes accessed | tf_op | source)
XLA Modules:
  0.0 91.9 jit_solution(8169023241960657607)
XLA Ops:
  0.6 0.0 copy-start.2
  0.6 0.0 copy-start.3
  0.7 0.0 copy-start.6
  0.7 1.2 %fusion = (f32[3,128,128]{2,1,0:T(8,128)S(1)}, f32[3,128,128]{2,1,0:T(8,128)S(1)}) fusion(f32[4,128,128]{2,1,0:T(8,128)} %doping_hbm.1), kind=kLoop, calls=%fused_computation.3 | loop fusion | bytes 786432 | tf_op jit(solution)/shard_map/halo_above/slice | solution.py:389
  1.9 1.0 %fusion.1 = (f32[2,128,128]{2,1,0:T(8,128)S(1)}, f32[2,128,128]{2,1,0:T(8,128)S(1)}) fusion(f32[4,128,128]{2,1,0:T(8,128)} %screening_hbm.1), kind=kLoop, calls=%fused_computation.4 | loop fusion | bytes 524288 | tf_op jit(solution)/shard_map/halo_above/slice | solution.py:389
  2.9 0.7 pad_maximum_fusion
  3.6 4.1 %collective-permute-start = (f32[5,128,128]{2,1,0:T(8,128)}, f32[5,128,128]{2,1,0:T(8,128)S(1)}, u32[]{:S(2)}, u32[]{:S(2)}) collective-permute-start(f32[5,128,128]{2,1,0:T(8,128)} %pad_maximum_fusion), channel_id=1, source_target_pairs={{0,1},{1,2},{2,3},{3,4},{4,5},{5,6},{6,7},{7,8},{8,9},{9,10},{10,1... | collective-permute-start | bytes 983048 | tf_op jit(solution)/shard_map/halo_below/ppermute | solution.py:387
  7.7 0.7 pad_maximum_fusion.1
  8.5 0.0 collective-permute-start.1
  8.5 0.1 pad_add_fusion.place
  8.5 0.0 copy-done.2
  8.6 0.0 copy-done.3
  8.6 0.0 copy-done.6
  8.6 0.0 copy-start.7
  8.6 0.9 %copy-done.7 = f32[256,256]{1,0:T(8,128)S(1)} copy-done((f32[256,256]{1,0:T(8,128)S(1)}, f32[256,256]{1,0:T(8,128)}, u32[]{:S(2)}) %copy-start.7) | copy-done | bytes 262168
  9.5 0.0 copy-start
  9.5 0.0 copy-start.1
  9.5 12.7 %chain.1 = (f32[264,128]{1,0:T(8,128)S(1)}, f32[8,256]{1,0:T(8,128)S(1)}, f32[2,256,256]{2,1,0:T(8,128)S(1)}, bf16[2,256,256]{2,1,0:T(8,128)(2,1)S(1)}, bf16[2,2...) custom-call(s32[3]{0:T(128)S(1)} %pad_add_fusion.place, ...), custom_call_target="tpu_custom_call" | custom-call | flops 5000000000 | tf_op jit(solution)/shard_map/chain/pallas_call | solution.py:392
  22.2 0.0 collective-permute-done.below_ref
  22.2 0.0 collective-permute-done.1.above_ref
  22.2 7.4 %collective-permute-start.2 = (f32[264,128]{1,0:T(8,128)S(1)}, f32[264,128]{1,0:T(8,128)S(1)}, u32[]{:S(2)}, u32[]{:S(2)}) collective-permute-start(f32[264,128]{1,0:T(8,128)S(1)} %get-tuple-element.25), channel_id=1, source_target_pairs={{0,1},{1,0},{2,3},{3,2},{4,5},{5,4},{6,7},{7,6},{8,9},{9,8},{10,11... | collective-permute-start | bytes 405512 | tf_op jit(solution)/shard_map/ppermute | solution.py:418
  29.6 1.0 %collective-permute-done.2.received_ref = f32[264,128]{1,0:T(8,128)S(1)} collective-permute-done((f32[264,128]{1,0:T(8,128)S(1)}, f32[264,128]{1,0:T(8,128)S(1)}, u32[]{:S(2)}, u32[]{:S(2)}) %collective-permute-start.2) | collective-permute-done | bytes 135200 | tf_op jit(solution)/shard_map/ppermute | solution.py:418
  30.6 1.2 %hop_2.1 = f32[264,128]{1,0:T(8,128)S(1)} custom-call(s32[3]{0:T(128)S(1)} %pad_add_fusion.place, f32[264,128]{1,0:T(8,128)S(1)} %collective-permute-done.2.received_ref, f32[2,256,256]{2,1,0:T(8,128)S(1)} %get-tuple-element.26.state_ref, bf16[2,256,256]{2,1,0:T(8,128)(2,1)S(1)} %get-tuple-element.27.map_h, bf16[2,256,256]{2,1,0:T(8,128)(2,1)S(1)} %get-tuple-element.28.map_l), custom_call_target="tpu_custom_call" | custom-call | flops 200000000 | tf_op jit(solution)/shard_map/middle/hop_2/pallas_call | solution.py:410
  31.9 1.9 %collective-permute-start.3 = (f32[264,128]{1,0:T(8,128)S(1)}, f32[264,128]{1,0:T(8,128)S(1)}, u32[]{:S(2)}, u32[]{:S(2)}) collective-permute-start(f32[264,128]{1,0:T(8,128)S(1)} %hop_2.1), channel_id=1, source_target_pairs={{0,0},{1,2},{2,1},{3,3},{4,4},{5,6},{6,5},{7,7},{8,8},{9,10},{10,9... | collective-permute-start | bytes 405512 | tf_op jit(solution)/shard_map/middle/ppermute | solution.py:420
  33.8 0.0 copy-done
  33.8 0.0 copy-done.1
  33.8 0.7 grid.1
  34.5 0.0 copy-start.5
  34.5 1.7 %first.1.base_ref = f32[8,256]{1,0:T(8,128)S(1)} custom-call(s32[3]{0:T(128)S(1)} %pad_add_fusion.place, f32[264,128]{1,0:T(8,128)S(1)} %collective-permute-done.2.received_ref, f32[256,256]{1,0:T(8,128)S(1)} %bitcast.6, f32[256,256]{1,0:T(8,128)S(1)} %bitcast.8, f32[8,256]{1,0:T(8,128)S(1)} %get-tuple-element.29.base_ref, ...), custom_call_target="tpu_custom_call" | custom-call | flops 500000000 | tf_op jit(solution)/shard_map/first/pallas_call | solution.py:426
  36.2 3.5 %collective-permute-done.3.received_ref.second_ref = f32[264,128]{1,0:T(8,128)S(1)} collective-permute-done((f32[264,128]{1,0:T(8,128)S(1)}, f32[264,128]{1,0:T(8,128)S(1)}, u32[]{:S(2)}, u32[]{:S(2)}) %collective-permute-start.3) | collective-permute-done | bytes 135200 | tf_op jit(solution)/shard_map/middle/ppermute | solution.py:420
  39.7 1.2 %hop_1.1 = f32[264,128]{1,0:T(8,128)S(1)} custom-call(s32[3]{0:T(128)S(1)} %pad_add_fusion.place, f32[264,128]{1,0:T(8,128)S(1)} %collective-permute-done.3.received_ref.second_ref, f32[2,256,256]{2,1,0:T(8,128)S(1)} %get-tuple-element.26.state_ref, bf16[2,256,256]{2,1,0:T(8,128)(2,1)S(1)} %get-tuple-element.27.map_h, ...), custom_call_target="tpu_custom_call" | custom-call | flops 200000000 | tf_op jit(solution)/shard_map/hop_1/pallas_call | solution.py:410
  40.9 0.1 collective-permute-start.4
  41.7 0.0 copy-start.4
  41.7 0.7 collective-permute-done.4.third_ref
  42.4 0.0 copy-done.5
  42.4 1.7 %second.1 = f32[8,8,256]{2,1,0:T(8,128)S(1)} custom-call(s32[3]{0:T(128)S(1)} %pad_add_fusion.place, s32[1]{0:T(128)S(6)} %copy.12.slot, f32[64]{0:T(128)S(1)} %copy-done.5, f32[264,128]{1,0:T(8,128)S(1)} %collective-permute-done.4.third_ref, f32[264,128]{1,0:T(8,128)S(1)} %collective-permute-done.3.received_ref.second_ref, f32[8,256]{1,0:T(8,128)S(1)} %first.1.base_ref, ...), custom_call_target="tpu_custom_call" | custom-call | flops 500000000 | tf_op jit(solution)/shard_map/second/pallas_call | solution.py:433
  44.1 10.5 %all_to_all.15.pieces_ref = f32[8,8,256]{2,1,0:T(8,128)S(1)} all-to-all(f32[8,8,256]{2,1,0:T(8,128)S(1)} %second.1), channel_id=1, replica_groups=mesh['energy_0'=4,'energy_1'=2,'energy_2'=8,'layer_0'=2,'layer_1'=2] {'e..., dimensions={0} | all-to-all | bytes 131072 | tf_op jit(solution)/shard_map/all_to_all | solution.py:370
  54.6 15.6 %all_to_all.16.pieces_ref = f32[32,8,256]{2,1,0:T(8,128)S(1)} all-to-all(f32[32,8,256]{2,1,0:T(8,128)S(1)} %fan.1), channel_id=1, replica_groups=mesh['energy_0'=4,'energy_1'=2,'energy_2'=8,'layer_0'=2,'layer_1'=2] {'e..., dimensions={0} | all-to-all | bytes 524288 | tf_op jit(solution)/shard_map/all_to_all | solution.py:370
  70.2 0.0 copy-done.4
  70.2 2.1 %krylov.1 = (f32[8,256]{1,0:T(8,128)}, f32[4,4,128,128]{3,2,1,0:T(8,128)S(1)}, f32[256,1,128]{2,1,0:T(1,128)S(1)}) custom-call(s32[3]{0:T(128)S(1)} %pad_add_fusion.place, s32[32]{0:T(128)S(1)} %copy-done.4, f32[32,8,256]{2,1,0:T(8,128)S(1)} %all_to_all.16.pieces_ref, f32[10,128,128]{2,1,0:T(8,128)S(1)} %get-tuple-element.38.field_ref, ...), custom_call_target="tpu_custom_call" | custom-call | flops 1000000 | tf_op jit(solution)/shard_map/krylov/pallas_call | solution.py:444
  72.3 18.2 %all_to_all.17.sums_ref = f32[256,1,128]{2,1,0:T(1,128)S(1)} all-to-all(f32[256,1,128]{2,1,0:T(1,128)S(1)} %get-tuple-element.41), channel_id=1, replica_groups=mesh['energy_0'=4,'energy_1'=2,'energy_2'=8,'layer_0'=2,'layer_1'=2] {'e..., dimensions={0} | all-to-all | bytes 262144 | tf_op jit(solution)/shard_map/all_to_all | solution.py:370
  90.5 1.3 %finish.1 = (f32[4,128,128]{2,1,0:T(8,128)}, f32[4,128,128]{2,1,0:T(8,128)}) custom-call(f32[256,1,128]{2,1,0:T(1,128)S(1)} %all_to_all.17.sums_ref, f32[4,4,128,128]{3,2,1,0:T(8,128)S(1)} %get-tuple-element.42.basis_ref), custom_call_target="tpu_custom_call" | custom-call | flops 1000000 | tf_op jit(solution)/shard_map/finish/pallas_call | solution.py:452
  (1 shorter events, 0.0 us)
Async XLA Ops:
  0.6 7.9 %copy-start.2 = (f32[1,256,256]{2,1,0:T(8,128)S(1)}, f32[1,256,256]{2,1,0:T(8,128)}, u32[]{:S(2)}) copy-start(f32[1,256,256]{2,1,0:T(8,128)} %param.11) | copy-start | bytes 786436
  0.6 7.9 %copy-start.3 = (f32[1,256,256]{2,1,0:T(8,128)S(1)}, f32[1,256,256]{2,1,0:T(8,128)}, u32[]{:S(2)}) copy-start(f32[1,256,256]{2,1,0:T(8,128)} %param.12) | copy-start | bytes 786436
  0.7 7.9 %copy-start.6 = (f32[1,8,256,256]{3,2,1,0:T(8,128)S(1)}, f32[1,8,256,256]{3,2,1,0:T(8,128)}, u32[]{:S(2)}) copy-start(f32[1,8,256,256]{3,2,1,0:T(8,128)} %param.9) | copy-start | bytes 6291460
  3.6 18.6 %collective-permute-start = (f32[5,128,128]{2,1,0:T(8,128)}, f32[5,128,128]{2,1,0:T(8,128)S(1)}, u32[]{:S(2)}, u32[]{:S(2)}) collective-permute-start(f32[5,128,128]{2,1,0:T(8,128)} %pad_maximum_fusion), channel_id=1, source_target_pairs={{0,1},{1,2},{2,3},{3,4},{4,5},{5,6},{6,7},{7,8},{8,9},{9,10},{10,1... | collective-permute-start | bytes 983048 | tf_op jit(solution)/shard_map/halo_below/ppermute | solution.py:387
  8.5 13.8 %collective-permute-start.1 = (f32[5,128,128]{2,1,0:T(8,128)}, f32[5,128,128]{2,1,0:T(8,128)S(1)}, u32[]{:S(2)}, u32[]{:S(2)}) collective-permute-start(f32[5,128,128]{2,1,0:T(8,128)} %pad_maximum_fusion.1), channel_id=1, source_target_pairs={{1,0},{2,1},{3,2},{4,3},{5,4},{6,5},{7,6},{8,7},{9,8},{10,9},{11,1... | collective-permute-start | bytes 983048 | tf_op jit(solution)/shard_map/halo_above/ppermute | solution.py:390
  8.6 1.0 %copy-start.7 = (f32[256,256]{1,0:T(8,128)S(1)}, f32[256,256]{1,0:T(8,128)}, u32[]{:S(2)}) copy-start(f32[256,256]{1,0:T(8,128)} %t_hbm.1) | copy-start | bytes 786436
  9.5 24.3 %copy-start = (f32[4,128,128]{2,1,0:T(8,128)S(1)}, f32[4,128,128]{2,1,0:T(8,128)}, u32[]{:S(2)}) copy-start(f32[4,128,128]{2,1,0:T(8,128)} %doping_hbm.1) | copy-start | bytes 786436
  9.5 24.3 %copy-start.1 = (f32[4,128,128]{2,1,0:T(8,128)S(1)}, f32[4,128,128]{2,1,0:T(8,128)}, u32[]{:S(2)}) copy-start(f32[4,128,128]{2,1,0:T(8,128)} %screening_hbm.1) | copy-start | bytes 786436
  22.2 8.4 %collective-permute-start.2 = (f32[264,128]{1,0:T(8,128)S(1)}, f32[264,128]{1,0:T(8,128)S(1)}, u32[]{:S(2)}, u32[]{:S(2)}) collective-permute-start(f32[264,128]{1,0:T(8,128)S(1)} %get-tuple-element.25), channel_id=1, source_target_pairs={{0,1},{1,0},{2,3},{3,2},{4,5},{5,4},{6,7},{7,6},{8,9},{9,8},{10,11... | collective-permute-start | bytes 405512 | tf_op jit(solution)/shard_map/ppermute | solution.py:418
  31.9 7.8 %collective-permute-start.3 = (f32[264,128]{1,0:T(8,128)S(1)}, f32[264,128]{1,0:T(8,128)S(1)}, u32[]{:S(2)}, u32[]{:S(2)}) collective-permute-start(f32[264,128]{1,0:T(8,128)S(1)} %hop_2.1), channel_id=1, source_target_pairs={{0,0},{1,2},{2,1},{3,3},{4,4},{5,6},{6,5},{7,7},{8,8},{9,10},{10,9... | collective-permute-start | bytes 405512 | tf_op jit(solution)/shard_map/middle/ppermute | solution.py:420
  34.5 7.9 %copy-start.5 = (f32[64]{0:T(128)S(1)}, f32[64]{0:T(128)}, u32[]{:S(2)}) copy-start(f32[64]{0:T(128)} %weights.1) | copy-start | bytes 772
  40.9 1.4 %collective-permute-start.4 = (f32[264,128]{1,0:T(8,128)S(1)}, f32[264,128]{1,0:T(8,128)S(1)}, u32[]{:S(2)}, u32[]{:S(2)}) collective-permute-start(f32[264,128]{1,0:T(8,128)S(1)} %hop_1.1), channel_id=1, source_target_pairs={{0,1},{1,0},{2,3},{3,2},{4,5},{5,4},{6,7},{7,6},{8,9},{9,8},{10,11... | collective-permute-start | bytes 405512 | tf_op jit(solution)/shard_map/ppermute | solution.py:432
  41.7 28.6 %copy-start.4 = (s32[32]{0:T(128)S(1)}, s32[32]{0:T(128)}, u32[]{:S(2)}) copy-start(s32[32]{0:T(128)} %plane_of.1) | copy-start | bytes 388

commit v2 on v1

--- a/solution.py
+++ b/solution.py
@@ -69,11 +69,10 @@
     d_ref, t_ref, lead, ph, pw, arrived,
 ):
     layers = d_ref.shape[0]
-    copies = [pltpu.make_async_copy(t_hbm, t_ref, arrived.at[0])]
-    for layer in range(layers):
-        copies.append(
-            pltpu.make_async_copy(d_hbm.at[layer], d_ref.at[layer], arrived.at[1 + layer])
-        )
+    order = [layer for pair in zip(range(layers), reversed(range(layers))) for layer in pair]
+    copies = [pltpu.make_async_copy(t_hbm, t_ref, arrived.at[layers])]
+    for layer in order[:layers]:
+        copies.append(pltpu.make_async_copy(d_hbm.at[layer], d_ref.at[layer], arrived.at[layer]))
     for copy in copies:
         copy.start()
 
@@ -85,37 +84,39 @@
     def _():
         pltpu.make_async_copy(lead_r_hbm, lead, arrived.at[1 + layers]).start()
 
-    copies[0].wait()
+    for copy in copies[:3]:
+        copy.wait()
     coupling = halves(t_ref[...])
-    for layer in range(layers):
-        copies[1 + layer].wait()
-        inverse = d_ref[layer]
-        split = halves(inverse)
+    seen = set()
+    for step in range(layers):
+        if step == 1:
+            for copy in copies[3:]:
+                copy.wait()
         for side, dims in ((0, NN), (1, NT)):
-            high, low = halves(product(split, coupling, dims))
-            ph[side, layer] = high
-            pw[side, layer] = low
-        base_ref[layer : layer + 1, :] = -diagonal_row(inverse)
-
-    rows, cols = square_iota(d_ref.shape[1])
-    for side, first in ((0, 0), (1, layers - 1)):
-        state_ref[side] = d_ref[first]
-        base_ref[first : first + 1, :] += diagonal_row(d_ref[first])
-        start = (ph[side, first].astype(F32) + pw[side, first].astype(F32)).T
-        kh_ref[side, first], kl_ref[side, first] = halves(start)
-
-    @pl.loop(1, layers)
-    def _(step):
-        for side in (0, 1):
             layer = step if side == 0 else layers - 1 - step
             before = step - 1 if side == 0 else layers - step
-            move = (ph[side, layer], pw[side, layer])
-            carried = product((kh_ref[side, before], kl_ref[side, before]), move, NT)
-            kh_ref[side, layer], kl_ref[side, layer] = halves(carried)
-            half_way = product(move, halves(state_ref[side]), NN)
-            updated = d_ref[layer] + product(halves(half_way), move, NT)
-            state_ref[side] = updated
-            base_ref[pl.ds(layer, 1), :] += diagonal_row(updated)
+            inverse = d_ref[layer]
+            ph[side, step], pw[side, step] = halves(product(halves(inverse), coupling, dims))
+            move = (ph[side, step], pw[side, step])
+            if step == 0:
+                state_ref[side] = inverse
+                kh_ref[side, layer], kl_ref[side, layer] = halves(
+                    (move[0].astype(F32) + move[1].astype(F32)).T
+                )
+                row = jnp.zeros_like(base_ref[:1, :])
+            else:
+                carried = product((kh_ref[side, before], kl_ref[side, before]), move, NT)
+                kh_ref[side, layer], kl_ref[side, layer] = halves(carried)
+                half_way = product(move, halves(state_ref[side]), NN)
+                updated = inverse + product(halves(half_way), move, NT)
+                state_ref[side] = updated
+                row = diagonal_row(updated)
+                if layer not in seen:
+                    row = row - diagonal_row(inverse)
+            if layer in seen:
+                row = row + base_ref[layer : layer + 1, :]
+            base_ref[layer : layer + 1, :] = row
+            seen.add(layer)
 
     for side, last in ((0, layers - 1), (1, 0)):
         whole = (kh_ref[side, last].astype(F32) + kl_ref[side, last].astype(F32)).T
@@ -199,32 +200,28 @@
 DEPTH = 3
 
 
-def grid_kernel(
-    place, doping_hbm, screening_hbm, below_ref, above_ref, field_ref, screen_ref, arrived
-):
-    own, planes = doping_hbm.shape[0], field_ref.shape[0]
-    copies = [
-        pltpu.make_async_copy(doping_hbm, field_ref.at[pl.ds(DEPTH, own)], arrived.at[0]),
-        pltpu.make_async_copy(screening_hbm, screen_ref.at[pl.ds(DEPTH, own)], arrived.at[1]),
+def edges_kernel(
+    doping_hbm, screening_hbm, doping_ref, screening_ref, high_ref, low_ref, arrived
+):
+    own = doping_hbm.shape[0]
+    near = DEPTH - 1
+    moves = [
+        (doping_hbm, doping_ref),
+        (screening_hbm, screening_ref),
+        (doping_hbm.at[pl.ds(own - DEPTH, DEPTH)], high_ref.at[pl.ds(0, DEPTH)]),
+        (screening_hbm.at[pl.ds(own - near, near)], high_ref.at[pl.ds(DEPTH, near)]),
+        (doping_hbm.at[pl.ds(0, DEPTH)], low_ref.at[pl.ds(0, DEPTH)]),
+        (screening_hbm.at[pl.ds(0, near)], low_ref.at[pl.ds(DEPTH, near)]),
     ]
+    copies = [pltpu.make_async_copy(*move, arrived.at[i]) for i, move in enumerate(moves)]
     for copy in copies:
         copy.start()
-    inside_low = jnp.where(place[1] == 0, 0.0, 1.0)
-    inside_high = jnp.where(place[1] == place[2], 0.0, 1.0)
-    for i in range(DEPTH):
-        field_ref[i] = below_ref[i] * -inside_low
-        field_ref[planes - DEPTH + i] = above_ref[i] * -inside_high
-    for i in range(DEPTH - 1):
-        screen_ref[i + 1] = below_ref[DEPTH + i]
-        screen_ref[planes - DEPTH + i] = above_ref[DEPTH + i]
     for copy in copies:
         copy.wait()
-    for i in range(DEPTH, DEPTH + own):
-        field_ref[i] = -field_ref[i]
 
 
 def krylov_kernel(
-    place, plane_of, pieces_ref, field_ref, screen_ref,
+    place, plane_of, pieces_ref, doping_ref, screening_ref, below_ref, above_ref,
     own_rows_ref, basis_ref, sums_ref, src, one, two, density_ref,
 ):
     slab, last_slab = place[1], place[2]
@@ -237,10 +234,16 @@
         density_ref[segment * layers : (segment + 1) * layers, :] = rows
     own_rows_ref[...] = density_ref[pl.ds(pl.multiple_of(place[0] * layers, layers), layers), :]
     depth, own = DEPTH, basis_ref.shape[1]
-    y_cells, z_cells = field_ref.shape[1:]
+    y_cells, z_cells = doping_ref.shape[1:]
     rows, cols = square_iota(y_cells)
     orbitals = density_ref.shape[1]
-    src[...] = field_ref[...]
+    inside_low = jnp.where(slab == 0, 0.0, 1.0)
+    inside_high = jnp.where(slab == last_slab, 0.0, 1.0)
+    for i in range(depth):
+        src[i] = below_ref[i] * -inside_low
+        src[depth + own + i] = above_ref[i] * -inside_high
+    for i in range(own):
+        src[depth + i] = -doping_ref[i]
     first_plane = slab * own - depth
 
     @pl.loop(0, plane_of.shape[0])
@@ -264,6 +267,13 @@
             )
             src[at] = src[at] + (dot(high, pick) + (dot(low, pick) + dot(lowest, pick)))
 
+    def screen(i):
+        if i < depth:
+            return below_ref[i + 2]
+        if i < depth + own:
+            return screening_ref[i - depth]
+        return above_ref[i - own]
+
     def shifted_operator(ref, i):
         plane = ref[i]
         beside = ref[i - 1] + ref[i + 1]
@@ -271,10 +281,7 @@
         beside = beside + jnp.where(rows == y_cells - 1, 0.0, pltpu.roll(plane, y_cells - 1, 0))
         beside = beside + jnp.where(cols == 0, 0.0, pltpu.roll(plane, 1, 1))
         beside = beside + jnp.where(cols == z_cells - 1, 0.0, pltpu.roll(plane, z_cells - 1, 1))
-        return (screen_ref[i] + (6.0 - SHIFT)) * plane - beside
-
-    inside_low = jnp.where(slab == 0, 0.0, 1.0)
-    inside_high = jnp.where(slab == last_slab, 0.0, 1.0)
+        return (screen(i) + (6.0 - SHIFT)) * plane - beside
 
     def masked(i, plane):
         if i < depth:
@@ -380,15 +387,7 @@
     place = jnp.stack([lax.axis_index(LAYER), slab, jnp.int32(slabs - 1)]).astype(jnp.int32)
     own, ny, nz = doping.shape
 
-    up = [(i, (i + 1) % slabs) for i in range(slabs)]
-    down = [(j, i) for i, j in up]
-    with jax.named_scope("halo_below"):
-        edge = jnp.concatenate([doping[own - 3 :], screening[own - 2 :]])
-        below = lax.ppermute(edge, ENERGY_LAYER, up)
-    with jax.named_scope("halo_above"):
-        edge = jnp.concatenate([doping[:3], screening[:2]])
-        above = lax.ppermute(edge, ENERGY_LAYER, down)
-
+    far = functools.partial(pltpu.with_memory_space_constraint, memory_space=pltpu.HBM)
     send, base, state, map_h, map_l, kh, kl = call(
         chain_kernel,
         (
@@ -404,7 +403,7 @@
             pltpu.SemaphoreType.DMA((layers + 2,)),
         ],
         flops=5 * 10**9, name="chain",
-    )(place, inverse, coupling, left, right)
+    )(place, far(inverse), far(coupling), far(left), far(right))
 
     def hop(received, right_at):
         return call(
@@ -414,22 +413,29 @@
         )(place, received, state, map_h, map_l)
 
     swap = [(0, 1), (1, 0), (2, 3), (3, 2)]
-    send, below, above = lax.optimization_barrier((send, below, above))
     first = lax.ppermute(send, LAYER, swap)
     with jax.named_scope("middle"):
         second = lax.ppermute(hop(first, 2), LAYER, [(0, 0), (1, 2), (2, 1), (3, 3)])
-    field, screen = call(
-        grid_kernel, (shape(own + 6, ny, nz), shape(own + 6, ny, nz)),
-        [SMEM, HBM, HBM, VMEM, VMEM], [pltpu.SemaphoreType.DMA((2,))],
-        flops=2 * 10**8, name="grid",
-    )(place, doping, screening, below, above)
+    planes, screens, high_edge, low_edge = call(
+        edges_kernel,
+        (shape(own, ny, nz), shape(own, ny, nz), shape(5, ny, nz), shape(5, ny, nz)),
+        [HBM, HBM], [pltpu.SemaphoreType.DMA((6,))],
+        flops=10**8, name="edges",
+    )(far(doping), far(screening))
     once = call(
         first_kernel, shape(layers, size), [SMEM, VMEM, HBM, HBM, VMEM, VMEM, VMEM],
         [pltpu.VMEM((size, size), F32)],
         flops=5 * 10**8, name="first",
-    )(place, first, left, right, base, kh, kl)
-    second, once, field, screen = lax.optimization_barrier((second, once, field, screen))
+    )(place, first, far(left), far(right), base, kh, kl)
+    second, once, planes, screens, high_edge, low_edge = lax.optimization_barrier(
+        (second, once, planes, screens, high_edge, low_edge)
+    )
     third = lax.ppermute(hop(second, 1), LAYER, swap)
+    third, high_edge, low_edge = lax.optimization_barrier((third, high_edge, low_edge))
+    up = [(i, (i + 1) % slabs) for i in range(slabs)]
+    down = [(j, i) for i, j in up]
+    below = lax.ppermute(high_edge, ENERGY_LAYER, up)
+    above = lax.ppermute(low_edge, ENERGY_LAYER, down)
     partial = call(
         second_kernel, shape(lax.axis_size(DEEP), layers, size), [SMEM] * 3 + [VMEM] * 5,
         [pltpu.VMEM((size, size), F32), pltpu.VMEM((layers, size), F32)],
@@ -439,15 +445,16 @@
     fanned = call(
         fan_kernel, shape(lax.axis_size(ACROSS), layers, size), [VMEM], flops=10**6, name="fan"
     )(along_z)
+    fanned, below, above = lax.optimization_barrier((fanned, below, above))
     pieces = exchange(fanned, ACROSS)
 
     own_rows, basis, sums = call(
         krylov_kernel,
         (shape(layers, size), shape(4, own, ny, nz), shape(slabs, 1, nz)),
-        [SMEM, SMEM] + [VMEM] * 3,
+        [SMEM, SMEM] + [VMEM] * 5,
         [pltpu.VMEM((own + 6, ny, nz), F32)] * 3 + [pltpu.VMEM((plane_of.shape[0], size), F32)],
         flops=10**6, name="krylov",
-    )(place, plane_of, pieces, field, screen)
+    )(place, plane_of, pieces, planes, screens, below, above)
     all_sums = exchange(sums, ENERGY_LAYER)
     potential, residual = call(
         finish_kernel, (shape(own, ny, nz), shape(own, ny, nz)), [VMEM] * 2,

time: 92.1 us -> 85.5 us (0.928)
  blocking collectives: 44.4 us -> 51.3 us
  starting transfers between devices: 13.5 us -> 7.85 us
  local copies, waits for them, and re-layouts: 3.17 us -> 0.01 us
  Pallas kernels: 22.6 us -> 20.6 us
  other arithmetic: 1.57 us -> 0.08 us
  waiting for transfers between devices: 5.18 us -> 3.98 us
    all_to_all x3, blocking collectives: 44.4 us -> 51.3 us  [exchange(): return lax.all_to_all(copies, axis, 0, 0, tiled=True)]
    ppermute x1, starting transfers between devices: 7.39 us -> 3.29 us  [body(): first = lax.ppermute(send, LAYER, swap)]
    ppermute x2, starting transfers between devices: 4.12 us -> 1.28 us  [the longest x1 1.28 us: body(): below = lax.ppermute(high_edge, ENERGY_LAYER, up)]
    pallas_call x1, Pallas kernels: 12.7 us -> 9.88 us  [body(): call(chain_kernel, (shape(PACKED, HALF), shape(layers, size), shape(2, si...]
    slice x2 -> x0, local copies, waits for them, and re-layouts: 2.19 us -> none  [body(): edge = jnp.concatenate([doping[:3], screening[:2]])]
    ppermute x1, waiting for transfers between devices: 3.5 us -> 1.64 us  [body(): lax.ppermute(hop(first, 2), LAYER, [(0, 0), (1, 2), (2, 1), (3, 3)])]
    concatenate x2 -> x0, other arithmetic: 1.49 us -> none  [the longest x1 0.75 us: body(): edge = jnp.concatenate([doping[own - 3:], screening[own - 2:]])]
    ppermute x1, starting transfers between devices: 1.92 us -> 3.19 us  [body(): lax.ppermute(hop(first, 2), LAYER, [(0, 0), (1, 2), (2, 1), (3, 3)])]
  transfers between devices with their start and end apart: 5 -> 5, of which waited for: 3 -> 3; matrix products, arithmetic and copies ran while one was open for 1% -> 0% of each run, Pallas kernels for 16% -> 6%
where the time goes in v2:
time: 85.5 us; the launch traced here: 85.3 us
  blocking collectives  51.3 us (60%)
  Pallas kernels  20.6 us (24%)
  starting transfers between devices  7.85 us (9%)
  waiting for transfers between devices  3.98 us (5%)
  between operations  1.4 us (2%)
    all_to_all x3, blocking collectives, exchange(): return lax.all_to_all(copies, axis, 0, 0, tiled=True)  51.3 us
    pallas_call x1, Pallas kernels, body(): call(chain_kernel, (shape(PACKED, HALF), shape(layers, size), shape(2, si...  9.88 us
    ppermute x1, starting transfers between devices, body(): first = lax.ppermute(send, LAYER, swap)  3.29 us
    ppermute x1, starting transfers between devices, body(): lax.ppermute(hop(first, 2), LAYER, [(0, 0), (1, 2), (2, 1), (3, 3)])  3.19 us
    pallas_call x2, Pallas kernels, hop(): call(functools.partial(hop_kernel, right_at), shape(PACKED, HALF), [SMEM,...  2.47 us
    pallas_call x1, Pallas kernels, body(): call(krylov_kernel, (shape(layers, size), shape(4, own, ny, nz), shape(sl...  2.08 us
    pallas_call x1, Pallas kernels, body(): call(second_kernel, shape(lax.axis_size(DEEP), layers, size), [SMEM] * 3...  1.85 us
  transfers between devices with their start and end apart: 5, of which 3 were waited for; matrix products, arithmetic and copies ran while one was open for 0% of the time, Pallas kernels for 6%

profile of v2, /device:TPU:1, one launch (start us, length us, event | category | flops | bytes accessed | tf_op | source)
XLA Modules:
  0.0 85.3 jit_solution(5352571386122585812)
XLA Ops:
  0.6 0.1 pad_add_fusion.place
  0.7 9.9 %chain.1 = (f32[264,128]{1,0:T(8,128)S(1)}, f32[8,256]{1,0:T(8,128)S(1)}, f32[2,256,256]{2,1,0:T(8,128)S(1)}, bf16[2,256,256]{2,1,0:T(8,128)(2,1)S(1)}, bf16[2,2...) custom-call(s32[3]{0:T(128)S(1)} %pad_add_fusion.place, ...), custom_call_target="tpu_custom_call" | custom-call | flops 5000000000 | tf_op jit(solution)/shard_map/chain/pallas_call | solution.py:391
  10.6 3.3 %collective-permute-start = (f32[264,128]{1,0:T(8,128)S(1)}, f32[264,128]{1,0:T(8,128)S(1)}, u32[]{:S(2)}, u32[]{:S(2)}) collective-permute-start(f32[264,128]{1,0:T(8,128)S(1)} %get-tuple-element.31), channel_id=1, source_target_pairs={{0,1},{1,0},{2,3},{3,2},{4,5},{5,4},{6,7},{7,6},{8,9},{9,8},{10,11... | collective-permute-start | bytes 405512 | tf_op jit(solution)/shard_map/ppermute | solution.py:416
  13.9 1.0 %collective-permute-done.received_ref = f32[264,128]{1,0:T(8,128)S(1)} collective-permute-done((f32[264,128]{1,0:T(8,128)S(1)}, f32[264,128]{1,0:T(8,128)S(1)}, u32[]{:S(2)}, u32[]{:S(2)}) %collective-permute-start) | collective-permute-done | bytes 135200 | tf_op jit(solution)/shard_map/ppermute | solution.py:416
  14.9 1.2 %hop_2.1 = f32[264,128]{1,0:T(8,128)S(1)} custom-call(s32[3]{0:T(128)S(1)} %pad_add_fusion.place, f32[264,128]{1,0:T(8,128)S(1)} %collective-permute-done.received_ref, f32[2,256,256]{2,1,0:T(8,128)S(1)} %get-tuple-element.32.state_ref, bf16[2,256,256]{2,1,0:T(8,128)(2,1)S(1)} %get-tuple-element.33.map_h, bf16[2,256,256]{2,1,0:T(8,128)(2,1)S(1)} %get-tuple-element.34.map_l), custom_call_target="tpu_custom_call" | custom-call | flops 200000000 | tf_op jit(solution)/shard_map/middle/hop_2/pallas_call | solution.py:409
  16.1 3.2 %collective-permute-start.1 = (f32[264,128]{1,0:T(8,128)S(1)}, f32[264,128]{1,0:T(8,128)S(1)}, u32[]{:S(2)}, u32[]{:S(2)}) collective-permute-start(f32[264,128]{1,0:T(8,128)S(1)} %hop_2.1), channel_id=1, source_target_pairs={{0,0},{1,2},{2,1},{3,3},{4,4},{5,6},{6,5},{7,7},{8,8},{9,10},{10,9... | collective-permute-start | bytes 405512 | tf_op jit(solution)/shard_map/middle/ppermute | solution.py:418
  19.3 1.3 %edges.1 = (f32[4,128,128]{2,1,0:T(8,128)S(1)}, f32[4,128,128]{2,1,0:T(8,128)S(1)}, f32[5,128,128]{2,1,0:T(8,128)S(1)}, f32[5,128,128]{2,1,0:T(8,128)S(1)}) custom-call(f32[4,128,128]{2,1,0:T(8,128)} %doping_hbm.1, f32[4,128,128]{2,1,0:T(8,128)} %screening_hbm.1), custom_call_target="tpu_custom_call" | custom-call | flops 100000000 | tf_op jit(solution)/shard_map/edges/pallas_call | solution.py:419
  20.6 0.0 copy-start.1
  20.6 1.7 %first.1.base_ref = f32[8,256]{1,0:T(8,128)S(1)} custom-call(s32[3]{0:T(128)S(1)} %pad_add_fusion.place, f32[264,128]{1,0:T(8,128)S(1)} %collective-permute-done.received_ref, f32[256,256]{1,0:T(8,128)} %bitcast.6, f32[256,256]{1,0:T(8,128)} %bitcast.8, f32[8,256]{1,0:T(8,128)S(1)} %get-tuple-element.35.base_ref, ...), custom_call_target="tpu_custom_call" | custom-call | flops 500000000 | tf_op jit(solution)/shard_map/first/pallas_call | solution.py:425
  22.3 1.6 %collective-permute-done.1.received_ref.second_ref = f32[264,128]{1,0:T(8,128)S(1)} collective-permute-done((f32[264,128]{1,0:T(8,128)S(1)}, f32[264,128]{1,0:T(8,128)S(1)}, u32[]{:S(2)}, u32[]{:S(2)}) %collective-permute-start.1) | collective-permute-done | bytes 135200 | tf_op jit(solution)/shard_map/middle/ppermute | solution.py:418
  24.0 1.2 %hop_1.1 = f32[264,128]{1,0:T(8,128)S(1)} custom-call(s32[3]{0:T(128)S(1)} %pad_add_fusion.place, f32[264,128]{1,0:T(8,128)S(1)} %collective-permute-done.1.received_ref.second_ref, f32[2,256,256]{2,1,0:T(8,128)S(1)} %get-tuple-element.32.state_ref, bf16[2,256,256]{2,1,0:T(8,128)(2,1)S(1)} %get-tuple-element.33.map_h, ...), custom_call_target="tpu_custom_call" | custom-call | flops 200000000 | tf_op jit(solution)/shard_map/hop_1/pallas_call | solution.py:409
  25.2 0.1 collective-permute-start.2
  25.3 1.3 %collective-permute-done.2.third_ref = f32[264,128]{1,0:T(8,128)S(1)} collective-permute-done((f32[264,128]{1,0:T(8,128)S(1)}, f32[264,128]{1,0:T(8,128)S(1)}, u32[]{:S(2)}, u32[]{:S(2)}) %collective-permute-start.2) | collective-permute-done | bytes 135200 | tf_op jit(solution)/shard_map/ppermute | solution.py:433
  26.6 1.3 %collective-permute-start.3 = (f32[5,128,128]{2,1,0:T(8,128)S(1)}, f32[5,128,128]{2,1,0:T(8,128)S(1)}, u32[]{:S(2)}, u32[]{:S(2)}) collective-permute-start(f32[5,128,128]{2,1,0:T(8,128)S(1)} %get-tuple-element.47), channel_id=1, source_target_pairs={{0,1},{1,2},{2,3},{3,4},{4,5},{5,6},{6,7},{7,8},{8,9},{9,10},{10,1... | collective-permute-start | bytes 983048 | tf_op jit(solution)/shard_map/ppermute | solution.py:437
  27.9 0.0 collective-permute-start.4
  28.6 0.0 copy-done.1
  28.6 0.0 copy-start
  28.6 1.8 %second.1 = f32[8,8,256]{2,1,0:T(8,128)S(1)} custom-call(s32[3]{0:T(128)S(1)} %pad_add_fusion.place, s32[1]{0:T(128)S(6)} %copy.12.slot, f32[64]{0:T(128)S(1)} %copy-done.1, f32[264,128]{1,0:T(8,128)S(1)} %collective-permute-done.2.third_ref, f32[264,128]{1,0:T(8,128)S(1)} %collective-permute-done.1.received_ref.second_ref, f32[8,256]{1,0:T(8,128)S(1)} %first.1.base_ref, ...), custom_call_target="tpu_custom_call" | custom-call | flops 500000000 | tf_op jit(solution)/shard_map/second/pallas_call | solution.py:439
  30.4 15.2 %all_to_all.15.pieces_ref = f32[8,8,256]{2,1,0:T(8,128)S(1)} all-to-all(f32[8,8,256]{2,1,0:T(8,128)S(1)} %second.1), channel_id=1, replica_groups=mesh['energy_0'=4,'energy_1'=2,'energy_2'=8,'layer_0'=2,'layer_1'=2] {'e..., dimensions={0} | all-to-all | bytes 131072 | tf_op jit(solution)/shard_map/all_to_all | solution.py:377
  45.7 0.0 collective-permute-done.3.below_ref
  45.7 0.0 collective-permute-done.4.above_ref
  45.7 17.9 %all_to_all.16.pieces_ref = f32[32,8,256]{2,1,0:T(8,128)S(1)} all-to-all(f32[32,8,256]{2,1,0:T(8,128)S(1)} %fan.1), channel_id=1, replica_groups=mesh['energy_0'=4,'energy_1'=2,'energy_2'=8,'layer_0'=2,'layer_1'=2] {'e..., dimensions={0} | all-to-all | bytes 524288 | tf_op jit(solution)/shard_map/all_to_all | solution.py:377
  63.6 0.0 copy-done
  63.6 2.1 %krylov.1 = (f32[8,256]{1,0:T(8,128)}, f32[4,4,128,128]{3,2,1,0:T(8,128)S(1)}, f32[256,1,128]{2,1,0:T(1,128)S(1)}) custom-call(s32[3]{0:T(128)S(1)} %pad_add_fusion.place, s32[32]{0:T(128)S(1)} %copy-done, f32[32,8,256]{2,1,0:T(8,128)S(1)} %all_to_all.16.pieces_ref, f32[4,128,128]{2,1,0:T(8,128)S(1)} %get-tuple-element.50.doping_ref, ...), custom_call_target="tpu_custom_call" | custom-call | flops 1000000 | tf_op jit(solution)/shard_map/krylov/pallas_call | solution.py:451
  65.7 18.2 %all_to_all.17.sums_ref = f32[256,1,128]{2,1,0:T(1,128)S(1)} all-to-all(f32[256,1,128]{2,1,0:T(1,128)S(1)} %get-tuple-element.55), channel_id=1, replica_groups=mesh['energy_0'=4,'energy_1'=2,'energy_2'=8,'layer_0'=2,'layer_1'=2] {'e..., dimensions={0} | all-to-all | bytes 262144 | tf_op jit(solution)/shard_map/all_to_all | solution.py:377
  83.9 1.3 %finish.1 = (f32[4,128,128]{2,1,0:T(8,128)}, f32[4,128,128]{2,1,0:T(8,128)}) custom-call(f32[256,1,128]{2,1,0:T(1,128)S(1)} %all_to_all.17.sums_ref, f32[4,4,128,128]{3,2,1,0:T(8,128)S(1)} %get-tuple-element.56.basis_ref), custom_call_target="tpu_custom_call" | custom-call | flops 1000000 | tf_op jit(solution)/shard_map/finish/pallas_call | solution.py:459
  (1 shorter events, 0.0 us)
Async XLA Ops:
  10.6 4.3 %collective-permute-start = (f32[264,128]{1,0:T(8,128)S(1)}, f32[264,128]{1,0:T(8,128)S(1)}, u32[]{:S(2)}, u32[]{:S(2)}) collective-permute-start(f32[264,128]{1,0:T(8,128)S(1)} %get-tuple-element.31), channel_id=1, source_target_pairs={{0,1},{1,0},{2,3},{3,2},{4,5},{5,4},{6,7},{7,6},{8,9},{9,8},{10,11... | collective-permute-start | bytes 405512 | tf_op jit(solution)/shard_map/ppermute | solution.py:416
  16.1 7.8 %collective-permute-start.1 = (f32[264,128]{1,0:T(8,128)S(1)}, f32[264,128]{1,0:T(8,128)S(1)}, u32[]{:S(2)}, u32[]{:S(2)}) collective-permute-start(f32[264,128]{1,0:T(8,128)S(1)} %hop_2.1), channel_id=1, source_target_pairs={{0,0},{1,2},{2,1},{3,3},{4,4},{5,6},{6,5},{7,7},{8,8},{9,10},{10,9... | collective-permute-start | bytes 405512 | tf_op jit(solution)/shard_map/middle/ppermute | solution.py:418
  20.6 8.0 %copy-start.1 = (f32[64]{0:T(128)S(1)}, f32[64]{0:T(128)}, u32[]{:S(2)}) copy-start(f32[64]{0:T(128)} %weights.1) | copy-start | bytes 772
  25.2 1.4 %collective-permute-start.2 = (f32[264,128]{1,0:T(8,128)S(1)}, f32[264,128]{1,0:T(8,128)S(1)}, u32[]{:S(2)}, u32[]{:S(2)}) collective-permute-start(f32[264,128]{1,0:T(8,128)S(1)} %hop_1.1), channel_id=1, source_target_pairs={{0,1},{1,0},{2,3},{3,2},{4,5},{5,4},{6,7},{7,6},{8,9},{9,8},{10,11... | collective-permute-start | bytes 405512 | tf_op jit(solution)/shard_map/ppermute | solution.py:433
  26.6 19.1 %collective-permute-start.3 = (f32[5,128,128]{2,1,0:T(8,128)S(1)}, f32[5,128,128]{2,1,0:T(8,128)S(1)}, u32[]{:S(2)}, u32[]{:S(2)}) collective-permute-start(f32[5,128,128]{2,1,0:T(8,128)S(1)} %get-tuple-element.47), channel_id=1, source_target_pairs={{0,1},{1,2},{2,3},{3,4},{4,5},{5,6},{6,7},{7,8},{8,9},{9,10},{10,1... | collective-permute-start | bytes 983048 | tf_op jit(solution)/shard_map/ppermute | solution.py:437
  27.9 17.8 %collective-permute-start.4 = (f32[5,128,128]{2,1,0:T(8,128)S(1)}, f32[5,128,128]{2,1,0:T(8,128)S(1)}, u32[]{:S(2)}, u32[]{:S(2)}) collective-permute-start(f32[5,128,128]{2,1,0:T(8,128)S(1)} %get-tuple-element.48), channel_id=1, source_target_pairs={{1,0},{2,1},{3,2},{4,3},{5,4},{6,5},{7,6},{8,7},{9,8},{10,9},{11,1... | collective-permute-start | bytes 983048 | tf_op jit(solution)/shard_map/ppermute | solution.py:438
  28.6 35.0 %copy-start = (s32[32]{0:T(128)S(1)}, s32[32]{0:T(128)}, u32[]{:S(2)}) copy-start(s32[32]{0:T(128)} %plane_of.1) | copy-start | bytes 388
